TPU v7x, 8 devices: a whole 2x2x1 slice. The times are simulated.
8 devices in a mesh: dp: 2 (over z, y), tp: 4 (over x, core).
Axes of the slice: x: 2, y: 2, z: 1, core: 2. Of those that a mesh axis runs over, the one named last changes fastest.
Arguments:
- x: bfloat16 [2, 128, 2560], P('dp', 'tp'), parts along dimension 0
- ln1_gamma: float32 [2560], replicated
- ln1_beta: float32 [2560], replicated
- w_qkv: bfloat16 [2560, 32, 3, 80], P(None, 'tp')
- b_qkv: float32 [32, 3, 80], P('tp')
- w_out: bfloat16 [2560, 2560], P('tp')
- b_out: float32 [2560], replicated
- ln2_gamma: float32 [2560], replicated
- ln2_beta: float32 [2560], replicated
- w_up: bfloat16 [2560, 10240], P(None, 'tp')
- b_up: float32 [10240], P('tp')
- w_down: bfloat16 [10240, 2560], P('tp')
- b_down: float32 [2560], replicated
- grad_y: bfloat16 [2, 128, 2560], P('dp', 'tp'), parts along dimension 0
Outputs:
- output 1: bfloat16 [2, 128, 2560], P('dp', 'tp'), parts along dimension 0
- output 2: bfloat16 [2, 128, 2560], P('dp', 'tp'), parts along dimension 0
- output 3: float32 [5120], P('dp'), parts along dimension 0
- output 4: float32 [5120], P('dp'), parts along dimension 0
- output 5: bfloat16 [5120, 32, 3, 80], P('dp', 'tp'), parts along dimension 0
- output 6: float32 [64, 3, 80], P(('dp', 'tp')), parts along dimension 0
- output 7: bfloat16 [5120, 2560], P(('dp', 'tp')), parts along dimension 0
- output 8: float32 [5120], P('dp'), parts along dimension 0
- output 9: float32 [5120], P('dp'), parts along dimension 0
- output 10: float32 [5120], P('dp'), parts along dimension 0
- output 11: bfloat16 [5120, 10240], P('dp', 'tp'), parts along dimension 0
- output 12: float32 [20480], P(('dp', 'tp')), parts along dimension 0
- output 13: bfloat16 [20480, 2560], P(('dp', 'tp')), parts along dimension 0
- output 14: float32 [5120], P('dp'), parts along dimension 0
There are 2 independent parts. A program takes and returns all parts, laid end to end along the dimension named above; an argument that names none is the same for every part.
All inputs are finite; a program needn't handle non-finite values.
Results may differ from a plain program's by a relative error of at most 0.0177361.
Values are sent between devices in bfloat16 or wider.
A program may use at most 1 GiB of HBM per device.

v0:
```python
import math
import jax
import jax.numpy as jnp
from jax import lax
from jax.sharding import PartitionSpec as P

EPS = 1e-5
MASK_VALUE = -1e30


def alibi_slopes(n_heads):
    closest = 2 ** int(math.floor(math.log2(n_heads)))
    base_ratio = 2.0 ** (-8.0 / closest)
    extra_ratio = 2.0 ** (-4.0 / closest)
    remaining = min(closest, n_heads - closest)
    slopes = [base_ratio ** (i + 1) for i in range(closest)]
    slopes = slopes + [extra_ratio ** (2 * i + 1) for i in range(remaining)]
    return jnp.array(slopes, dtype=jnp.float32)


def layer_norm(values, ln_gain, ln_bias):
    row_mean = jnp.mean(values, axis=-1, keepdims=True)
    centered = values - row_mean
    variance = jnp.mean(centered * centered, axis=-1, keepdims=True)
    return centered * lax.rsqrt(variance + EPS) * ln_gain + ln_bias


def gelu_tanh(values):
    return jax.nn.gelu(values, approximate=True)


def seq_gather(values):
    return lax.all_gather(values, 'tp', axis=1, tiled=True)


def seq_reduce(values):
    return lax.psum_scatter(values, 'tp', scatter_dimension=1, tiled=True)


def solution(mesh):
    tp_size = mesh.shape['tp']

    def local_step(x, ln1_gamma, ln1_beta, w_qkv, b_qkv, w_out, b_out, ln2_gamma, ln2_beta, w_up, b_up, w_down, b_down, grad_y):
        batch_size, seq_local = x.shape[0], x.shape[1]
        local_heads, head_size = w_qkv.shape[1], w_qkv.shape[3]
        seq_full = seq_local * tp_size
        score_scale = head_size ** -0.5
        tp_index = lax.axis_index('tp')
        slopes = lax.dynamic_slice_in_dim(alibi_slopes(local_heads * tp_size), tp_index * local_heads, local_heads)
        positions = jnp.arange(seq_full)
        causal = positions[None, :] <= positions[:, None]
        alibi_bias = slopes[:, None] * positions.astype(jnp.float32)[None, :]

        x_f = x.astype(jnp.float32)
        h_full = seq_gather(layer_norm(x_f, ln1_gamma, ln1_beta).astype(jnp.bfloat16))
        qkv_vals = (jnp.einsum('bsd,dhte->bshte', h_full, w_qkv, preferred_element_type=jnp.float32) + b_qkv).astype(jnp.bfloat16)
        q_heads = qkv_vals[:, :, :, 0]
        k_heads = qkv_vals[:, :, :, 1]
        v_heads = qkv_vals[:, :, :, 2]
        scores = jnp.einsum('bihe,bjhe->bhij', q_heads, k_heads, preferred_element_type=jnp.float32) * score_scale + alibi_bias[None, :, None, :]
        prob_f = jax.nn.softmax(jnp.where(causal, scores, MASK_VALUE), axis=-1)
        prob_bf = prob_f.astype(jnp.bfloat16)
        context = jnp.einsum('bhij,bjhe->bihe', prob_bf, v_heads, preferred_element_type=jnp.float32).astype(jnp.bfloat16)
        context_flat = context.reshape(batch_size, seq_full, local_heads * head_size)
        attn_out = seq_reduce(jnp.einsum('bsc,cd->bsd', context_flat, w_out, preferred_element_type=jnp.float32).astype(jnp.bfloat16))
        x_mid = x_f + attn_out.astype(jnp.float32) + b_out
        g_full = seq_gather(layer_norm(x_mid, ln2_gamma, ln2_beta).astype(jnp.bfloat16))
        pre_act = jnp.einsum('bsd,df->bsf', g_full, w_up, preferred_element_type=jnp.float32) + b_up
        activated = gelu_tanh(pre_act).astype(jnp.bfloat16)
        mlp_out = seq_reduce(jnp.einsum('bsf,fd->bsd', activated, w_down, preferred_element_type=jnp.float32).astype(jnp.bfloat16))
        y = (x_mid + mlp_out.astype(jnp.float32) + b_down).astype(jnp.bfloat16)

        grad_y_f = grad_y.astype(jnp.float32)
        grad_b_down = lax.psum(jnp.sum(grad_y_f, axis=(0, 1)), 'tp')
        grad_m_full = seq_gather(grad_y)
        grad_w_down = jnp.einsum('bsf,bsd->fd', activated, grad_m_full, preferred_element_type=jnp.float32).astype(jnp.bfloat16)
        grad_act = jnp.einsum('bsd,fd->bsf', grad_m_full, w_down, preferred_element_type=jnp.float32).astype(jnp.bfloat16)
        _, gelu_pullback = jax.vjp(gelu_tanh, pre_act)
        grad_pre = gelu_pullback(grad_act.astype(jnp.float32))[0]
        grad_b_up = jnp.sum(grad_pre, axis=(0, 1))
        grad_pre_bf = grad_pre.astype(jnp.bfloat16)
        grad_w_up = jnp.einsum('bsd,bsf->df', g_full, grad_pre_bf, preferred_element_type=jnp.float32).astype(jnp.bfloat16)
        grad_g = seq_reduce(jnp.einsum('bsf,df->bsd', grad_pre_bf, w_up, preferred_element_type=jnp.float32).astype(jnp.bfloat16))
        _, ln2_pullback = jax.vjp(layer_norm, x_mid, ln2_gamma, ln2_beta)
        grad_mid_ln, grad_ln2_gamma, grad_ln2_beta = ln2_pullback(grad_g.astype(jnp.float32))
        grad_ln2_gamma = lax.psum(grad_ln2_gamma, 'tp')
        grad_ln2_beta = lax.psum(grad_ln2_beta, 'tp')
        grad_mid = grad_y_f + grad_mid_ln
        grad_b_out = lax.psum(jnp.sum(grad_mid, axis=(0, 1)), 'tp')
        grad_attn_full = seq_gather(grad_mid.astype(jnp.bfloat16))
        grad_w_out = jnp.einsum('bsc,bsd->cd', context_flat, grad_attn_full, preferred_element_type=jnp.float32).astype(jnp.bfloat16)
        grad_context = jnp.einsum('bsd,cd->bsc', grad_attn_full, w_out, preferred_element_type=jnp.float32).astype(jnp.bfloat16)
        grad_context = grad_context.reshape(batch_size, seq_full, local_heads, head_size)
        grad_prob = jnp.einsum('bihe,bjhe->bhij', grad_context, v_heads, preferred_element_type=jnp.float32).astype(jnp.bfloat16).astype(jnp.float32)
        grad_v = jnp.einsum('bhij,bihe->bjhe', prob_bf, grad_context, preferred_element_type=jnp.float32).astype(jnp.bfloat16)
        grad_scores = prob_f * (grad_prob - jnp.sum(grad_prob * prob_f, axis=-1, keepdims=True))
        grad_scores_bf = grad_scores.astype(jnp.bfloat16)
        grad_q = (jnp.einsum('bhij,bjhe->bihe', grad_scores_bf, k_heads, preferred_element_type=jnp.float32) * score_scale).astype(jnp.bfloat16)
        grad_k = (jnp.einsum('bhij,bihe->bjhe', grad_scores_bf, q_heads, preferred_element_type=jnp.float32) * score_scale).astype(jnp.bfloat16)
        grad_qkv = jnp.stack([grad_q, grad_k, grad_v], axis=3)
        grad_b_qkv = jnp.sum(grad_qkv, axis=(0, 1), dtype=jnp.float32)
        grad_w_qkv = jnp.einsum('bsd,bshte->dhte', h_full, grad_qkv, preferred_element_type=jnp.float32).astype(jnp.bfloat16)
        grad_h = seq_reduce(jnp.einsum('bshte,dhte->bsd', grad_qkv, w_qkv, preferred_element_type=jnp.float32).astype(jnp.bfloat16))
        _, ln1_pullback = jax.vjp(layer_norm, x_f, ln1_gamma, ln1_beta)
        grad_x_ln, grad_ln1_gamma, grad_ln1_beta = ln1_pullback(grad_h.astype(jnp.float32))
        grad_ln1_gamma = lax.psum(grad_ln1_gamma, 'tp')
        grad_ln1_beta = lax.psum(grad_ln1_beta, 'tp')
        grad_x = (grad_mid + grad_x_ln).astype(jnp.bfloat16)
        return (y, grad_x, grad_ln1_gamma, grad_ln1_beta, grad_w_qkv, grad_b_qkv, grad_w_out, grad_b_out,
                grad_ln2_gamma, grad_ln2_beta, grad_w_up, grad_b_up, grad_w_down, grad_b_down)

    row_spec = P('dp', 'tp', None)
    in_specs = (row_spec, P(), P(), P(None, 'tp', None, None), P('tp', None, None), P('tp', None), P(), P(), P(),
                P(None, 'tp'), P('tp'), P('tp', None), P(), row_spec)
    out_specs = (row_spec, row_spec, P('dp'), P('dp'), P('dp', 'tp', None, None), P(('dp', 'tp'), None, None),
                 P(('dp', 'tp'), None), P('dp'), P('dp'), P('dp'), P('dp', 'tp'), P(('dp', 'tp')), P(('dp', 'tp'), None), P('dp'))
    return jax.shard_map(local_step, mesh=mesh, in_specs=in_specs, out_specs=out_specs, check_vma=False)
```

profile of v0, /device:TPU:0, one launch (start us, length us, event | category | flops | bytes accessed | tf_op | source)
XLA Modules:
  0.0 199.9 jit_solution(12091759757345539273)
XLA Ops:
  7.3 1.2 convert_reduce_fusion.3
  8.5 1.1 fusion.45
  9.6 1.1 fusion.43
  10.7 12.4 %all_gather.12 = bf16[1,128,2560]{2,1,0:T(8,128)(2,1)} all-gather(bf16[1,32,2560]{2,1,0:T(8,128)(2,1)S(1)} %fusion.43), channel_id=1, replica_groups=mesh['dp'=2,'tp'=4] {'tp'}, dimensions={1}, use_global_device_ids=true | all-gather | bytes 819200 | tf_op jit(solution)/shard_map/all_gather | solution.py:33
  23.1 5.5 %fusion.31 = f32[128,1920]{0,1:S(1)} fusion(bf16[2560,1920]{0,1:T(8,128)(2,1)} %bitcast.116, bf16[1,128,2560]{2,1,0:T(8,128)(2,1)} %all_gather.12), kind=kOutput, calls=%fused_computation.52 | convolution fusion | flops 1258291200 | bytes 11468800
  28.7 1.1 fusion.33
  29.9 2.2 %fusion.66 = (f32[8,128]{1,0:T(8,128)S(1)}, f32[8,128,128]{1,2,0:T(8,128)}) fusion(f32[8,128]{1,0:T(8,128)S(1)} %broadcast_multiply_fusion, pred[128,128]{0,1:T(8,128)(4,1)S(1)} %iota_compare_fusion, bf16[1,128,8,3,80]{1,4,3,2,0:T(8,128)(2,1)} %fusion.33), kind=kOutput, calls=%fused_computation.122 | convolution fusion | flops 21627008 | bytes 876544 | tf_op jit(solution)/shard_map/sub | solution.py:61
  32.1 1.4 convolution_convert_fusion.9
  33.5 0.7 copy-done.14
  34.2 1.5 fusion.6
  35.8 10.7 %all_gather.14 = bf16[1,128,2560]{2,1,0:T(8,128)(2,1)} all-gather(bf16[1,32,2560]{2,1,0:T(8,128)(2,1)} %param.28), channel_id=1, replica_groups=mesh['dp'=2,'tp'=4] {'tp'}, dimensions={1}, use_global_device_ids=true | all-gather | bytes 819200 | tf_op jit(solution)/shard_map/all_gather | solution.py:33
  46.6 6.8 %reduce-scatter.5.cloned.1.call-done = bf16[1,32,2560]{2,1,0:T(8,128)(2,1)} async-done(((bf16[1,128,2560]{2,1,0:T(8,128)(2,1)}), bf16[1,32,2560]{2,1,0:T(8,128)(2,1)}) %reduce-scatter.5.cloned.1.call-update) | async-done | bytes 163856 | tf_op jit(solution)/shard_map/reduce_scatter | solution.py:37
  53.3 1.1 fusion.53
  54.4 1.1 multiply_reduce_fusion.1
  55.6 1.0 add_convert_fusion.3
  56.6 10.4 %all_gather.13 = bf16[1,128,2560]{2,1,0:T(8,128)(2,1)S(1)} all-gather(bf16[1,32,2560]{2,1,0:T(8,128)(2,1)S(1)} %add_convert_fusion.3), channel_id=1, replica_groups=mesh['dp'=2,'tp'=4] {'tp'}, dimensions={1}, use_global_device_ids=true | all-gather | bytes 819200 | tf_op jit(solution)/shard_map/all_gather | solution.py:33
  67.0 0.9 copy-done.3
  67.9 6.7 %convolution_add_fusion = f32[128,2560]{1,0:T(8,128)S(1)} fusion(bf16[2560,2560]{1,0:T(8,128)(2,1)} %param.24, bf16[1,128,2560]{2,1,0:T(8,128)(2,1)S(1)} %all_gather.13, f32[2560]{0:T(1024)S(1)} %copy-done.23), kind=kOutput, calls=%fused_computation.5 | convolution fusion | flops 1678049280 | bytes 15083520 | tf_op jit(solution)/shard_map/bsd,df->bsf/dot_general | solution.py:68
  74.5 10.4 %fusion.67 = (f32[2560]{0:T(1024)}, bf16[128,2560]{1,0:T(8,128)(2,1)S(1)}) fusion(f32[128,2560]{1,0:T(8,128)S(1)} %convolution_add_fusion, bf16[2560,2560]{1,0:T(8,128)(2,1)} %param.26, bf16[1,128,2560]{2,1,0:T(8,128)(2,1)S(1)} %copy-done.12), kind=kOutput, calls=%fused_computation.123 | convolution fusion | flops 1685255680 | bytes 15738880 | tf_op jit(solution)/shard_map/bsd,fd->bsf/dot_general | solution.py:77
  84.9 0.9 copy-done.10
  85.8 9.8 %fusion.4 = bf16[1,128,2560]{2,1,0:T(8,128)(2,1)} fusion(bf16[2560,2560]{1,0:T(8,128)(2,1)} %param.24, bf16[128,2560]{1,0:T(8,128)(2,1)S(1)} %get-tuple-element.37), kind=kOutput, calls=%fused_computation.13 | convolution fusion | flops 1678049280 | bytes 14417920 | tf_op jit(solution)/shard_map/bsf,df->bsd/dot_general | solution.py:83
  95.7 8.0 %fusion.3 = bf16[1,128,2560]{2,1,0:T(8,128)(2,1)} fusion(bf16[2560,2560]{1,0:T(8,128)(2,1)} %param.26, f32[128,2560]{1,0:T(8,128)} %copy-done.6), kind=kOutput, calls=%fused_computation.12 | convolution fusion | flops 1680998400 | bytes 15073280 | tf_op jit(solution)/shard_map/bsf,fd->bsd/dot_general | solution.py:70
  103.9 10.1 %convolution_convert_fusion = bf16[2560,2560]{1,0:T(8,128)(2,1)} fusion(bf16[1,128,2560]{2,1,0:T(8,128)(2,1)} %all_gather.14, f32[128,2560]{1,0:T(8,128)} %copy-done.6), kind=kOutput, calls=%fused_computation.1 | convolution fusion | flops 1687224320 | bytes 15073280 | tf_op jit(solution)/shard_map/bsf,bsd->fd/dot_general | solution.py:76
  114.0 1.2 convert_reduce_fusion.2
  115.3 1.3 fusion.48
  116.6 0.5 negate_multiply_fusion.1
  117.1 15.4 %reduce-scatter.7.cloned.1.call-done = bf16[1,32,2560]{2,1,0:T(8,128)(2,1)} async-done(((bf16[1,128,2560]{2,1,0:T(8,128)(2,1)}), bf16[1,32,2560]{2,1,0:T(8,128)(2,1)}) %reduce-scatter.7.cloned.1.call-update) | async-done | bytes 163856 | tf_op jit(solution)/shard_map/reduce_scatter | solution.py:37
  132.5 2.1 %fusion.65 = (f32[2560]{0:T(1024)S(1)}, f32[1,32,2560]{2,1,0:T(8,128)S(1)}, bf16[1,32,2560]{2,1,0:T(8,128)(2,1)}, f32[2560]{0:T(1024)S(1)}) fusion(f32[32]{0:T(128)} %negate_multiply_fusion.1, f32[32]{0:T(128)S(1)} %multiply_multiply_fusion.3, f32[32]{0:T(128)S(1)} %broadcast_multiply_fusion.1, f32[2560]{0:T(1024)S(1)} %copy-done.17, ...), kind=kLoop, calls=%fused_computation.121 | loop fusion | flops 1633280 | bytes 1362432 | tf_op jit(solution)/shard_map/reduce_sum | solution.py:89
  134.6 0.7 copy-done.9
  135.3 10.4 %all_gather.15 = bf16[1,128,2560]{2,1,0:T(8,128)(2,1)S(1)} all-gather(bf16[1,32,2560]{2,1,0:T(8,128)(2,1)S(1)} %convert_element_type.190), channel_id=1, replica_groups=mesh['dp'=2,'tp'=4] {'tp'}, dimensions={1}, use_global_device_ids=true | all-gather | bytes 819200 | tf_op jit(solution)/shard_map/all_gather | solution.py:33
  145.7 0.8 copy-done.7
  146.5 1.8 convolution_convert_fusion.10
  148.3 1.1 copy.40
  149.5 1.5 multiply_reduce_fusion
  151.0 0.2 fusion.22
  151.3 0.3 fusion.21
  151.6 0.3 fusion.20
  151.9 6.3 %fusion.5 = bf16[1,128,2560]{2,1,0:T(8,128)(2,1)} fusion(bf16[2560,8,3,80]{0,3,2,1:T(8,128)(2,1)} %param.18, bf16[1,128,8,1,80]{1,4,2,3,0:T(8,128)(2,1)S(1)} %fusion.20, bf16[1,128,8,1,80]{1,4,2,3,0:T(8,128)(2,1)S(1)} %fusion.21, bf16[1,128,8,1,80]{1,4,2,3,0:T(8,128)(2,1)S(1)} %fusion.22), kind=kOutput, calls=%fused_computation.14 | convolution fusion | flops 1259110400 | bytes 10977280 | tf_op jit(solution)/shard_map/bshte,dhte->bsd/dot_general | solution.py:103
  158.3 6.9 %convolution_convert_fusion.1 = bf16[2560,2560]{1,0:T(8,128)(2,1)} fusion(bf16[1,128,2560]{2,1,0:T(8,128)(2,1)S(1)} %copy-done.4, bf16[128,2560]{1,0:T(8,128)(2,1)S(1)} %copy-done.11), kind=kOutput, calls=%fused_computation.2 | convolution fusion | flops 1684275200 | bytes 14417920 | tf_op jit(solution)/shard_map/bsd,bsf->df/dot_general | solution.py:82
  165.2 1.0 copy-done.5
  166.2 2.7 %fusion.29 = f32[2560,1920]{0,1:S(1)} fusion(bf16[128,1920]{0,1:T(8,128)(2,1)S(1)} %bitcast.118, bf16[1,128,2560]{2,1,0:T(8,128)(2,1)S(1)} %copy-done.5), kind=kOutput, calls=%fused_computation.50 | convolution fusion | flops 1258291200 | bytes 20807680
  168.9 4.6 %convert_element_type.208 = bf16[2560,8,3,80]{0,3,2,1:T(8,128)(2,1)} convert(f32[2560,8,3,80]{0,3,2,1:T(8,128)S(1)} %bitcast.115) | non-fusion elementwise | flops 4915200 | bytes 29491200 | tf_op jit(solution)/shard_map/convert_element_type | solution.py:102
  173.6 0.9 convert_reduce_fusion
  174.5 2.7 %convolution_convert_fusion.2 = bf16[640,2560]{1,0:T(8,128)(2,1)} fusion(bf16[128,640]{0,1:T(8,128)(2,1)S(1)} %bitcast.120, bf16[1,128,2560]{2,1,0:T(8,128)(2,1)S(1)} %copy-done.8), kind=kOutput, calls=%fused_computation.3 | convolution fusion | flops 421068800 | bytes 4096000 | tf_op jit(solution)/shard_map/bsc,bsd->cd/dot_general | solution.py:91
  177.2 1.1 convert_reduce_fusion.1
  178.3 1.3 fusion.49
  179.7 11.9 %all-reduce = (f32[2560]{0:T(1024)}, f32[2560]{0:T(1024)}, f32[2560]{0:T(1024)}, f32[2560]{0:T(1024)}, f32[2560]{0:T(1024)}, /*index=5*/f32[2560]{0:T(1024)}) all-reduce(f32[2560]{0:T(1024)S(1)} %get-tuple-element.16, f32[2560]{0:T(1024)S(1)} %get-tuple-element.20, ...), channel_id=1, replica_groups=mesh['dp'=2,'tp'=4] {'tp'}, use_global_device_ids=true, to_apply=%region_16.17 | all-reduce | flops 15360 | bytes 122880 | tf_op jit(solution)/shard_map/psum | solution.py:106
  191.6 1.8 add_convert_fusion.1
  (70 shorter events, 0.9 us)
Async XLA Ops:
  7.2 27.0 %copy-start = (bf16[640,2560]{1,0:T(8,128)(2,1)S(1)}, bf16[640,2560]{1,0:T(8,128)(2,1)}, u32[]{:S(2)}) copy-start(bf16[640,2560]{1,0:T(8,128)(2,1)} %param.20) | copy-start | bytes 9830404
  7.2 15.9 %copy-start.21 = (f32[8,3,80]{2,0,1:T(8,128)S(1)}, f32[8,3,80]{2,0,1:T(8,128)}, u32[]{:S(2)}) copy-start(f32[8,3,80]{2,0,1:T(8,128)} %param.19) | copy-start | bytes 23044
  7.2 46.1 %reduce-scatter.5.cloned.1.call-start = ((), (), s32[]{:S(2)}) async-start(), calls=%async_computation.4 | async-start | bytes 819200 | tf_op jit(solution)/shard_map/reduce_scatter | solution.py:37
  28.7 1.1 copy-start.24
  33.5 0.7 copy-start.14
  35.7 17.6 %copy-start.2 = (bf16[1,32,2560]{2,1,0:T(8,128)(2,1)S(1)}, bf16[1,32,2560]{2,1,0:T(8,128)(2,1)}, u32[]{:S(2)}) copy-start(bf16[1,32,2560]{2,1,0:T(8,128)(2,1)} %param.15) | copy-start | bytes 491524
  35.7 17.6 %copy-start.17 = (f32[2560]{0:T(1024)S(1)}, f32[2560]{0:T(1024)}, u32[]{:S(2)}) copy-start(f32[2560]{0:T(1024)} %param.21) | copy-start | bytes 30724
  35.7 19.8 %copy-start.19 = (f32[2560]{0:T(1024)S(1)}, f32[2560]{0:T(1024)}, u32[]{:S(2)}) copy-start(f32[2560]{0:T(1024)} %param.22) | copy-start | bytes 30724
  35.7 19.8 %copy-start.22 = (f32[2560]{0:T(1024)S(1)}, f32[2560]{0:T(1024)}, u32[]{:S(2)}) copy-start(f32[2560]{0:T(1024)} %param.23) | copy-start | bytes 30724
  35.8 32.1 %copy-start.23 = (f32[2560]{0:T(1024)S(1)}, f32[2560]{0:T(1024)}, u32[]{:S(2)}) copy-start(f32[2560]{0:T(1024)} %param.25) | copy-start | bytes 30724
  35.8 78.2 %reduce-scatter.9.cloned.1.call-start = ((), (), s32[]{:S(2)}) async-start(), calls=%async_computation.6 | async-start | bytes 819200 | tf_op jit(solution)/shard_map/reduce_scatter | solution.py:37
  67.0 0.9 copy-start.3
  67.9 6.7 %copy-start.12 = (bf16[1,128,2560]{2,1,0:T(8,128)(2,1)S(1)}, bf16[1,128,2560]{2,1,0:T(8,128)(2,1)}, u32[]{:S(2)}) copy-start(bf16[1,128,2560]{2,1,0:T(8,128)(2,1)} %all_gather.14) | copy-start | bytes 1966084
  74.5 10.4 %copy-start.6 = (f32[128,2560]{1,0:T(8,128)}, f32[128,2560]{1,0:T(8,128)S(1)}, u32[]{:S(2)}) copy-start(f32[128,2560]{1,0:T(8,128)S(1)} %convolution_add_fusion) | copy-start | bytes 3932164
  84.9 0.9 copy-start.10
  95.6 36.9 %reduce-scatter.7.cloned.1.call-start = ((), (), s32[]{:S(2)}) async-start(), calls=%async_computation.5 | async-start | bytes 819200 | tf_op jit(solution)/shard_map/reduce_scatter | solution.py:37
  103.7 28.8 %copy-start.20 = (f32[2560]{0:T(1024)S(1)}, f32[2560]{0:T(1024)}, u32[]{:S(2)}) copy-start(f32[2560]{0:T(1024)} %param.27) | copy-start | bytes 30724
  103.7 73.5 %reduce-scatter.11.cloned.1.call-start = ((), (), s32[]{:S(2)}) async-start(), calls=%async_computation.7 | async-start | bytes 819200 | tf_op jit(solution)/shard_map/reduce_scatter | solution.py:37
  134.6 0.7 copy-start.9
  145.7 0.8 copy-start.7
  148.3 2.6 %copy-start.16 = (f32[8,128,128]{1,2,0:T(8,128)S(1)}, f32[8,128,128]{1,2,0:T(8,128)}, u32[]{:S(2)}) copy-start(f32[8,128,128]{1,2,0:T(8,128)} %get-tuple-element.33) | copy-start | bytes 1572868
  149.4 1.6 copy-start.13
  151.9 6.3 %copy-start.4 = (bf16[1,128,2560]{2,1,0:T(8,128)(2,1)S(1)}, bf16[1,128,2560]{2,1,0:T(8,128)(2,1)}, u32[]{:S(2)}) copy-start(bf16[1,128,2560]{2,1,0:T(8,128)(2,1)} %copy-done.3) | copy-start | bytes 1966084
  151.9 6.3 %copy-start.11 = (bf16[128,2560]{1,0:T(8,128)(2,1)S(1)}, bf16[128,2560]{1,0:T(8,128)(2,1)}, u32[]{:S(2)}) copy-start(bf16[128,2560]{1,0:T(8,128)(2,1)} %copy-done.10) | copy-start | bytes 1966084
  165.1 1.1 copy-start.5
  168.9 5.5 %copy-start.8 = (bf16[1,128,2560]{2,1,0:T(8,128)(2,1)S(1)}, bf16[1,128,2560]{2,1,0:T(8,128)(2,1)}, u32[]{:S(2)}) copy-start(bf16[1,128,2560]{2,1,0:T(8,128)(2,1)} %copy-done.7) | copy-start | bytes 1966084
  168.9 5.5 %copy-start.15 = (bf16[8,80,128]{2,1,0:T(8,128)(2,1)S(1)}, bf16[8,80,128]{2,1,0:T(8,128)(2,1)}, u32[]{:S(2)}) copy-start(bf16[8,80,128]{2,1,0:T(8,128)(2,1)} %copy-done.14) | copy-start | bytes 491524
  174.5 2.7 %copy-start.18 = (f32[2560]{0:T(1024)S(1)}, f32[2560]{0:T(1024)}, u32[]{:S(2)}) copy-start(f32[2560]{0:T(1024)} %param.16) | copy-start | bytes 30724
  174.5 18.9 %copy-start.1 = (bf16[640,2560]{1,0:T(8,128)(2,1)S(1)}, bf16[640,2560]{1,0:T(8,128)(2,1)}, u32[]{:S(2)}) copy-start(bf16[640,2560]{1,0:T(8,128)(2,1)} %param.20) | copy-start | bytes 9830404
Sparse Core Ops, SparseCore 0:
  35.9 17.4 reduce-scatter.4
  95.7 16.8 reduce-scatter.8
  115.7 16.7 reduce-scatter.6
  158.4 16.9 reduce-scatter.10
where the time goes:
time: 201 us; the launch traced here: 200 us
  matrix products  78.2 us (39%)
  blocking collectives  55.8 us (28%)
  other arithmetic  23 us (11%)
  waiting for transfers between devices  22.2 us (11%)
  between operations  14.1 us (7%)
  local copies, waits for them, and re-layouts  6.25 us (3%)
    all_gather x4, blocking collectives, seq_gather(): return lax.all_gather(values, 'tp', axis=1, tiled=True)  43.9 us
    reduce_scatter x4, waiting for transfers between devices, seq_reduce(): return lax.psum_scatter(values, 'tp', scatter_dimension=1, tiled=True)  22.2 us
    psum x1, blocking collectives, local_step(): grad_ln1_gamma = lax.psum(grad_ln1_gamma, 'tp')  11.9 us
    dot_general x1, matrix products, local_step(): jnp.einsum('bsd,fd->bsf', grad_m_full, w_down, preferred_element_type=jnp...  10.4 us
    dot_general x1, matrix products, local_step(): jnp.einsum('bsf,bsd->fd', activated, grad_m_full, preferred_element_type=...  10.1 us
    dot_general x1, matrix products, local_step(): jnp.einsum('bsf,df->bsd', grad_pre_bf, w_up, preferred_element_type=jnp.f...  9.82 us
    unnamed x2, matrix products  8.24 us
    dot_general x1, matrix products, local_step(): jnp.einsum('bsf,fd->bsd', activated, w_down, preferred_element_type=jnp.f...  8 us
  transfers between devices with their start and end apart: 4, of which 2 were waited for; matrix products, arithmetic and copies ran while one was open for 20% of the time, Pallas kernels for 0%

commit v1 on v0

v1 whole, which is shorter than its diff:
```python
import functools
import math
import jax
import jax.numpy as jnp
from jax import lax
from jax.experimental import pallas as pl
from jax.experimental.pallas import tpu as pltpu
from jax.sharding import PartitionSpec as P

EPS = 1e-5
MASK_VALUE = -1e30
BF = jnp.bfloat16
F32 = jnp.float32
MESH = pl.DeviceIdType.MESH
GELU_C = math.sqrt(2.0 / math.pi)
GELU_A = 0.044715
TP = 4
NCH = 5
LANES = 128


def alibi_slopes(n_heads):
    closest = 2 ** int(math.floor(math.log2(n_heads)))
    base_ratio = 2.0 ** (-8.0 / closest)
    extra_ratio = 2.0 ** (-4.0 / closest)
    remaining = min(closest, n_heads - closest)
    slopes = [base_ratio ** (i + 1) for i in range(closest)]
    return slopes + [extra_ratio ** (2 * i + 1) for i in range(remaining)]


def dot(lhs, rhs):
    return lax.dot_general(lhs, rhs, (((1,), (0,)), ((), ())), preferred_element_type=F32)


def dot_t(lhs, rhs):
    return lax.dot_general(lhs, rhs, (((1,), (1,)), ((), ())), preferred_element_type=F32)


def layer_kernel(x_h, gy_h, wqkv_h, bqkv_h, wout_h, wup_h, wdn_h, ln1g_h, ln1b_h, ln2g_h, ln2b_h, bout_h, bdown_h, bup_h,
                 y_o, gx_o, vec_o, h_o, ga_o, dpre_o, gy_o, dqkv_o, ctx_o, gt_o, rt_o,
                 wqkv, wout, wup, wdn, bqkv, vecs, xg, gyg, h, bias, qkv, prob, probb, ctx, x1, xhat, g, gt, rt, gact, r, dpre,
                 gmid, ga, dctx, dqkv, ybuf, gxbuf, xh1, vec, part,
                 p1, rd1, s1, rs1, t1, p2, rd2, s2, rs2, t2, py, rdy, sy, rsy, ph, rdh, sh, rsh,
                 lsem, osem, ssem, rsem):
    D = x_h.shape[1]
    seq = TP * 32
    head = bqkv_h.shape[2]
    n_heads = bqkv_h.shape[1]
    cw = D // NCH
    nlc = D // LANES
    t = lax.axis_index('tp')
    core = lax.rem(t, 2)
    chip = t // 2
    sib = t + 1 - 2 * core
    cross = lax.rem(t + 2, TP)
    sibcross = lax.rem(sib + 2, TP)

    def slot(dev):
        return lax.rem(dev, 2) * 2 + dev // 2

    def rows(dev):
        return pl.ds(pl.multiple_of(slot(dev) * 32, 32), 32)

    own = rows(t)
    half = pl.ds(pl.multiple_of(core * 64, 64), 64)
    sibhalf = pl.ds(pl.multiple_of((1 - core) * 64, 64), 64)
    blk_own = pl.ds(pl.multiple_of(chip * 32, 32), 32)
    blk_cross = pl.ds(pl.multiple_of((1 - chip) * 32, 32), 32)

    counter = [0, 0, 0]

    def load(src, dst):
        k = counter[0]
        counter[0] += 1
        copy = pltpu.make_async_copy(src, dst, lsem.at[k])
        copy.start()
        return copy

    outs = []

    def store(src, dst):
        k = counter[1]
        counter[1] += 1
        copy = pltpu.make_async_copy(src, dst, osem.at[k])
        copy.start()
        outs.append(copy)

    sent = []

    def remote(src, dst, dev):
        k = counter[2]
        counter[2] += 1
        copy = pltpu.make_async_remote_copy(src_ref=src, dst_ref=dst, send_sem=ssem.at[k], recv_sem=rsem.at[k],
                                            device_id={'tp': dev}, device_id_type=MESH)
        copy.start()
        sent.append(copy)
        return copy

    def lc(c):
        return slice(c * LANES, (c + 1) * LANES)

    def ch(j):
        return slice(j * cw, (j + 1) * cw)

    lx = load(x_h, xg.at[own, :])
    lg = load(gy_h, gyg.at[own, :])
    lvec = [load(src, vecs.at[k]) for k, src in enumerate((ln1g_h, ln1b_h, ln2g_h, ln2b_h, bout_h, bdown_h, bup_h))]
    lb = load(bqkv_h, bqkv)
    lwqkv = load(wqkv_h, wqkv)
    lwout = load(wout_h, wout)
    barrier = pltpu.get_barrier_semaphore()
    for dev in (sib, cross, sibcross):
        pl.semaphore_signal(barrier, inc=1, device_id={'tp': dev}, device_id_type=MESH)
    pl.semaphore_wait(barrier, 3)
    lx.wait()
    x_to_cross = remote(xg.at[own, :], xg.at[own, :], cross)
    x_to_sib = remote(xg.at[own, :], xg.at[own, :], sib)
    lg.wait()
    gy_to_sib = remote(gyg.at[own, :], gyg.at[own, :], sib)
    lwdn = load(wdn_h, wdn)
    lwup = load(wup_h, wup)
    for copy in lvec:
        copy.wait()

    def ln_block(rr, n, src, gain, shift, dst):
        acc = jnp.zeros((n, LANES), F32)
        for c in range(nlc):
            acc = acc + src[rr, lc(c)].astype(F32)
        mean = jnp.sum(acc, axis=1, keepdims=True) / D
        acc = jnp.zeros((n, LANES), F32)
        for c in range(nlc):
            z = src[rr, lc(c)].astype(F32) - mean
            acc = acc + z * z
        rstd = lax.rsqrt(jnp.sum(acc, axis=1, keepdims=True) / D + EPS)
        for c in range(nlc):
            z = (src[rr, lc(c)].astype(F32) - mean) * rstd
            if dst is not None:
                dst[rr, lc(c)] = (z * vecs[gain, :, lc(c)] + vecs[shift, :, lc(c)]).astype(BF)
            else:
                xh1[:, lc(c)] = z
        return rstd

    ln_block(own, 32, xg, 0, 1, h)
    lb.wait()
    for k in range(3):
        bt = bqkv[k].T
        for hd in range(n_heads):
            at = (hd * 3 + k) * head
            bias[at:at + head, :] = jnp.broadcast_to(bt[:head, hd:hd + 1], (head, seq))
    x_to_sib.wait_recv()
    ln_block(rows(sib), 32, xg, 0, 1, h)
    x_to_cross.wait_recv()
    x_fwd = remote(xg.at[rows(cross), :], xg.at[rows(cross), :], sib)
    gy_to_cross = remote(gyg.at[own, :], gyg.at[own, :], cross)
    ln_block(rows(cross), 32, xg, 0, 1, h)
    x_fwd.wait_recv()
    ln_block(rows(sibcross), 32, xg, 0, 1, h)
    lwqkv.wait()

    hr = 2 * 3 * head
    hv = h[...]
    for m in range(n_heads // 2):
        mm = slice(m * hr, (m + 1) * hr)
        qkv[mm, :] = (dot_t(wqkv[mm, :], hv) + bias[mm, :]).astype(BF)
    store(h, h_o)

    def position(axis):
        i = lax.broadcasted_iota(jnp.int32, (seq, seq), axis)
        b = i >> 5
        return ((((b & 1) << 1) | (b >> 1)) << 5) | (i & 31)

    pos_k = position(0)
    causal = pos_k <= position(1)
    key_f = pos_k.astype(F32)
    slopes = alibi_slopes(n_heads * TP)
    score_scale = head ** -0.5

    def part_of(hd, k):
        at = (hd * 3 + k) * head
        return slice(at, at + head)

    def slope(hd):
        v = jnp.float32(slopes[hd])
        for dev in range(1, TP):
            v = jnp.where(t == dev, jnp.float32(slopes[dev * n_heads + hd]), v)
        return v

    for hd in range(n_heads):
        s = dot(qkv[part_of(hd, 1), :].T, qkv[part_of(hd, 0), :]) * score_scale + slope(hd) * key_f
        s = jnp.where(causal, s, MASK_VALUE)
        e = jnp.exp(s - jnp.max(s, axis=0, keepdims=True))
        pr = e * (1.0 / jnp.sum(e, axis=0, keepdims=True))
        prob[hd] = pr
        probb[hd] = pr.astype(BF)
    for hd in range(n_heads):
        ctx[hd * head:(hd + 1) * head, :] = dot(qkv[part_of(hd, 2), :], probb[hd]).astype(BF)

    class AllSum:
        def __init__(self, p, rd, s, rs, tt):
            self.p, self.rd, self.s, self.rs, self.tt = p, rd, s, rs, tt
            self.a, self.b, self.c = {}, {}, {}

        def put(self, j, value):
            self.p[:, ch(j)] = value
            self.a[j] = remote(self.p.at[sibhalf, ch(j)], self.rd.at[:, ch(j)], sib)

        def step_cross(self, j):
            self.a[j].wait_recv()
            self.s[:, ch(j)] = (self.p[half, ch(j)].astype(F32) + self.rd[:, ch(j)].astype(F32)).astype(BF)
            self.b[j] = remote(self.s.at[:, ch(j)], self.rs.at[:, ch(j)], cross)

        def step_back(self, j):
            self.b[j].wait_recv()
            self.tt[half, ch(j)] = (self.s[:, ch(j)].astype(F32) + self.rs[:, ch(j)].astype(F32)).astype(BF)
            self.c[j] = remote(self.tt.at[half, ch(j)], self.tt.at[half, ch(j)], sib)

        def finish(self, j):
            self.c[j].wait_recv()

    class ScatterSum(AllSum):
        def step_cross(self, j):
            self.a[j].wait_recv()
            self.s[:, ch(j)] = (self.p[half, ch(j)].astype(F32) + self.rd[:, ch(j)].astype(F32)).astype(BF)
            self.b[j] = remote(self.s.at[blk_cross, ch(j)], self.rs.at[:, ch(j)], cross)

        def result(self, j, c):
            return (self.s[blk_own, c].astype(F32) + self.rs[:, c].astype(F32)).astype(BF).astype(F32)

    lwout.wait()
    o_flat = ctx[...].T
    sum_a = AllSum(p1, rd1, s1, rs1, t1)
    for j in range(NCH):
        sum_a.put(j, dot(o_flat, wout[:, ch(j)]).astype(BF))
        if j:
            sum_a.step_cross(j - 1)
    sum_a.step_cross(NCH - 1)
    store(ctx, ctx_o)

    gy_to_sib.wait_recv()
    gy_to_cross.wait_recv()
    gy_fwd = remote(gyg.at[rows(cross), :], gyg.at[rows(cross), :], sib)
    gy_fwd.wait_recv()
    store(gyg, gy_o)
    lwdn.wait()
    fw = wdn_h.shape[0] // NCH
    acc = jnp.zeros((seq, LANES), F32)

    def x1_chunk(j, acc):
        sum_a.finish(j)
        for c in range(j * (cw // LANES), (j + 1) * (cw // LANES)):
            z = xg[:, lc(c)].astype(F32) + t1[:, lc(c)].astype(F32) + vecs[4, :, lc(c)]
            x1[:, lc(c)] = z
            acc = acc + z
        return acc

    gyv = gyg[...]
    for j in range(NCH):
        ff = slice(j * fw, (j + 1) * fw)
        gact[:, ff] = dot_t(gyv, wdn[ff, :]).astype(BF)
        sum_a.step_back(j)
        if j:
            acc = x1_chunk(j - 1, acc)
    acc = x1_chunk(NCH - 1, acc)

    mean = jnp.sum(acc, axis=1, keepdims=True) / D
    acc = jnp.zeros((seq, LANES), F32)
    for c in range(nlc):
        z = x1[:, lc(c)] - mean
        acc = acc + z * z
    rstd2 = lax.rsqrt(jnp.sum(acc, axis=1, keepdims=True) / D + EPS)
    for c in range(nlc):
        z = (x1[:, lc(c)] - mean) * rstd2
        xhat[:, lc(c)] = z
        g[:, lc(c)] = (z * vecs[2, :, lc(c)] + vecs[3, :, lc(c)]).astype(BF)

    lwup.wait()
    gv = g[...]
    for j in range(NCH):
        ff = slice(j * fw, (j + 1) * fw)
        pre = dot(gv, wup[:, ff]) + vecs[6, :, ff]
        sq = pre * pre
        th = jnp.tanh(GELU_C * (pre + GELU_A * (pre * sq)))
        one = 0.5 * (1.0 + th)
        r[:, ff] = (pre * one).astype(BF)
        slope_g = one + 0.5 * pre * (1.0 - th * th) * (GELU_C * (1.0 + 3.0 * GELU_A * sq))
        gp = gact[:, ff].astype(F32) * slope_g
        vec[6:7, ff] = jnp.sum(gp, axis=0, keepdims=True)
        dpre[:, ff] = gp.astype(BF)

    dv = dpre[...]
    sum_g = AllSum(p2, rd2, s2, rs2, t2)
    for j in range(NCH):
        sum_g.put(j, dot_t(dv, wup[ch(j), :]).astype(BF))
        if j:
            sum_g.step_cross(j - 1)
    sum_g.step_cross(NCH - 1)
    store(dpre, dpre_o)

    acc1 = jnp.zeros((seq, LANES), F32)
    acc2 = jnp.zeros((seq, LANES), F32)

    def ln2_back_chunk(j, acc1, acc2):
        sum_g.finish(j)
        for c in range(j * (cw // LANES), (j + 1) * (cw // LANES)):
            dg = t2[:, lc(c)].astype(F32)
            z = xhat[:, lc(c)]
            dgz = dg * z
            vec[2:3, lc(c)] = jnp.sum(dgz, axis=0, keepdims=True)
            vec[3:4, lc(c)] = jnp.sum(dg, axis=0, keepdims=True)
            gain = vecs[2, :, lc(c)]
            acc1 = acc1 + dg * gain
            acc2 = acc2 + dgz * gain
        return acc1, acc2

    rv = r[...]
    sum_y = ScatterSum(py, rdy, sy, rsy, None)
    for j in range(NCH):
        py[:, ch(j)] = dot(rv, wdn[:, ch(j)]).astype(BF)
        for c in range(j * (cw // LANES), (j + 1) * (cw // LANES)):
            gt[lc(c), :] = g[:, lc(c)].T
            rt[lc(c), :] = r[:, lc(c)].T
            vec[5:6, lc(c)] = jnp.sum(gyg[:, lc(c)].astype(F32), axis=0, keepdims=True)
        sum_g.step_back(j)
        if j:
            acc1, acc2 = ln2_back_chunk(j - 1, acc1, acc2)
    acc1, acc2 = ln2_back_chunk(NCH - 1, acc1, acc2)

    mean1 = jnp.sum(acc1, axis=1, keepdims=True) / D
    mean2 = jnp.sum(acc2, axis=1, keepdims=True) / D
    for c in range(nlc):
        dz = t2[:, lc(c)].astype(F32) * vecs[2, :, lc(c)]
        gm = gyg[:, lc(c)].astype(F32) + rstd2 * (dz - mean1 - xhat[:, lc(c)] * mean2)
        gmid[:, lc(c)] = gm
        vec[4:5, lc(c)] = jnp.sum(gm, axis=0, keepdims=True)
        ga[:, lc(c)] = gm.astype(BF)

    y_sib = remote(py.at[sibhalf, :], rdy, sib)
    store(gt, gt_o)
    store(rt, rt_o)
    store(ga, ga_o)

    dctx[...] = dot_t(wout[...], ga[...]).astype(BF)
    for hd in range(n_heads):
        hh = slice(hd * head, (hd + 1) * head)
        do = dctx[hh, :]
        pr = prob[hd]
        dp = dot(qkv[part_of(hd, 2), :].T, do).astype(BF).astype(F32)
        dqkv[part_of(hd, 2), :] = dot_t(do, probb[hd]).astype(BF)
        ds = (pr * (dp - jnp.sum(dp * pr, axis=0, keepdims=True))).astype(BF)
        dqkv[part_of(hd, 0), :] = (dot(qkv[part_of(hd, 1), :], ds) * score_scale).astype(BF)
        dqkv[part_of(hd, 1), :] = (dot_t(qkv[part_of(hd, 0), :], ds) * score_scale).astype(BF)

    y_sib.wait_recv()
    sy[...] = (py[half, :].astype(F32) + rdy[...].astype(F32)).astype(BF)
    y_cross = remote(sy.at[blk_cross, :], rsy, cross)

    sum_h = ScatterSum(ph, rdh, sh, rsh, None)
    dq = dqkv[...].T
    for j in range(NCH):
        sum_h.put(j, dot(dq, wqkv[:, ch(j)]).astype(BF))
        if j:
            sum_h.step_cross(j - 1)
    sum_h.step_cross(NCH - 1)
    store(dqkv, dqkv_o)

    rstd1 = ln_block(own, 32, xg, 0, 1, None)
    y_cross.wait_recv()
    for c in range(nlc):
        z = (sy[blk_own, lc(c)].astype(F32) + rsy[:, lc(c)].astype(F32)).astype(BF).astype(F32)
        ybuf[:, lc(c)] = (x1[own, lc(c)] + z + vecs[5, :, lc(c)]).astype(BF)
    store(ybuf, y_o)

    me = slot(t)
    acc1 = jnp.zeros((32, LANES), F32)
    acc2 = jnp.zeros((32, LANES), F32)
    for j in range(NCH):
        sum_h.b[j].wait_recv()
        for c in range(j * (cw // LANES), (j + 1) * (cw // LANES)):
            dh = sum_h.result(j, lc(c))
            z = xh1[:, lc(c)]
            dhz = dh * z
            part[me, 0:1, lc(c)] = jnp.sum(dhz, axis=0, keepdims=True)
            part[me, 1:2, lc(c)] = jnp.sum(dh, axis=0, keepdims=True)
            gain = vecs[0, :, lc(c)]
            acc1 = acc1 + dh * gain
            acc2 = acc2 + dhz * gain
    parts = [remote(part.at[me], part.at[me], dev) for dev in (cross, sibcross, sib)]
    mean1 = jnp.sum(acc1, axis=1, keepdims=True) / D
    mean2 = jnp.sum(acc2, axis=1, keepdims=True) / D
    for c in range(nlc):
        dz = sum_h.result(None, lc(c)) * vecs[0, :, lc(c)]
        gxbuf[:, lc(c)] = (gmid[own, lc(c)] + rstd1 * (dz - mean1 - xh1[:, lc(c)] * mean2)).astype(BF)
    store(gxbuf, gx_o)
    for copy in parts:
        copy.wait_recv()
    vec[0:2, :] = (part[0] + part[1]) + (part[2] + part[3])
    store(vec, vec_o)
    for copy in sent:
        copy.wait_send()
    for copy in outs:
        copy.wait()


def grad_kernel(h_h, ga_h, dpre_h, gy_h, dqkv_h, ctx_h, gt_h, rt_h, vec_h, y_h, gx_h,
                dwqkv_o, dwout_o, dwup_o, dwdn_o, dbqkv_o, y_o, gx_o, v0, v1, v2, v3, v4, v5, v6,
                h, ga, dpre, gy, dqkv, ctx, gt, rt, vec, y, gx, buf, isem, osem):
    n_heads, head = dbqkv_o.shape[1], dbqkv_o.shape[2]
    block = 320
    slots = buf.shape[0]
    loads = []
    for k, (src, dst) in enumerate(((rt_h, rt), (gy_h, gy), (gt_h, gt), (dpre_h, dpre), (dqkv_h, dqkv), (h_h, h), (ctx_h, ctx),
                                    (ga_h, ga), (vec_h, vec), (y_h, y), (gx_h, gx))):
        copy = pltpu.make_async_copy(src, dst, isem.at[k])
        copy.start()
        loads.append(copy)

    step = 0
    pending = []
    for n, (left, right, out, la, lb) in enumerate(((rt, gy, dwdn_o, 0, 1), (gt, dpre, dwup_o, 2, 3), (dqkv, h, dwqkv_o, 4, 5),
                                                    (ctx, ga, dwout_o, 6, 7))):
        loads[la].wait()
        loads[lb].wait()
        rv = right[...]
        for m in range(left.shape[0] // block):
            s = step % slots
            if step >= slots:
                pending[step - slots].wait()
            mm = slice(m * block, (m + 1) * block)
            buf[s] = dot(left[mm, :], rv).astype(BF)
            copy = pltpu.make_async_copy(buf.at[s], out.at[pl.ds(m * block, block), :], osem.at[s])
            copy.start()
            pending.append(copy)
            step += 1
    ones = jnp.ones((8, dqkv.shape[1]), BF)
    sums = dot_t(ones, dqkv[...])[0:1]
    for k in range(3):
        for hd in range(n_heads):
            at = (hd * 3 + k) * head
            dbqkv_o[k, hd:hd + 1, :] = sums[:, at:at + head]
    for k in range(8, 11):
        loads[k].wait()
    y_o[...] = y[...]
    gx_o[...] = gx[...]
    for k, o in enumerate((v0, v1, v2, v3, v4, v5, v6)):
        o[...] = vec[k, :]
    for k in range(max(0, step - slots), step):
        pending[k].wait()


def solution(mesh):
    def local_step(x, ln1_gamma, ln1_beta, w_qkv, b_qkv, w_out, b_out, ln2_gamma, ln2_beta, w_up, b_up, w_down, b_down, grad_y):
        D = x.shape[2]
        S = TP * x.shape[1]
        nh, head = w_qkv.shape[1], w_qkv.shape[3]
        Q = nh * 3 * head
        C = nh * head
        FL = w_up.shape[1]
        any_spec = pl.BlockSpec(memory_space=pl.ANY)
        vm = pltpu.VMEM
        wqkv_t = jnp.transpose(w_qkv, (1, 2, 3, 0)).reshape(Q, D)
        bq = jnp.transpose(b_qkv, (1, 0, 2))
        sds = jax.ShapeDtypeStruct
        n_loads = 2 + 7 + 1 + 4
        n_remote = 64
        red = [vm((S, D), BF), vm((S // 2, D), BF), vm((S // 2, D), BF), vm((S // 2, D), BF), vm((S, D), BF)]
        scat = [vm((S, D), BF), vm((S // 2, D), BF), vm((S // 2, D), BF), vm((S // TP, D), BF)]
        row = lambda v: v.reshape(1, D)
        res = pl.pallas_call(
            layer_kernel,
            name='layer',
            out_shape=[sds((S // TP, D), BF), sds((S // TP, D), BF), sds((8, D), F32), sds((S, D), BF), sds((S, D), BF),
                       sds((S, FL), BF), sds((S, D), BF), sds((Q, S), BF), sds((C, S), BF), sds((D, S), BF), sds((FL, S), BF)],
            in_specs=[any_spec] * 14,
            out_specs=[any_spec] * 11,
            scratch_shapes=[
                vm((Q, D), BF), vm((C, D), BF), vm((D, FL), BF), vm((FL, D), BF), vm((3, nh, head), F32), vm((7, 1, D), F32),
                vm((S, D), BF), vm((S, D), BF), vm((S, D), BF), vm((Q, S), F32), vm((Q, S), BF), vm((nh, S, S), F32),
                vm((nh, S, S), BF), vm((C, S), BF), vm((S, D), F32), vm((S, D), F32), vm((S, D), BF), vm((D, S), BF), vm((FL, S), BF),
                vm((S, FL), BF), vm((S, FL), BF), vm((S, FL), BF), vm((S, D), F32), vm((S, D), BF), vm((C, S), BF), vm((Q, S), BF),
                vm((S // TP, D), BF), vm((S // TP, D), BF), vm((S // TP, D), F32), vm((8, D), F32), vm((TP, 2, D), F32),
                *red, *red, *scat, *scat,
                pltpu.SemaphoreType.DMA((n_loads,)), pltpu.SemaphoreType.DMA((16,)),
                pltpu.SemaphoreType.DMA((n_remote,)), pltpu.SemaphoreType.DMA((n_remote,)),
            ],
            compiler_params=pltpu.CompilerParams(collective_id=0, has_side_effects=True, vmem_limit_bytes=67043328),
        )(x.reshape(x.shape[1], D), grad_y.reshape(x.shape[1], D), wqkv_t, bq, w_out, w_up, w_down, row(ln1_gamma), row(ln1_beta),
          row(ln2_gamma), row(ln2_beta), row(b_out), row(b_down), row(b_up))
        y, gx, vec, h, ga, dpre, gyf, dqkv, ctx, gt, rt = res
        vspec = pl.BlockSpec(memory_space=pltpu.VMEM)
        vshape = sds((D,), F32)
        outs = pl.pallas_call(
            grad_kernel,
            name='weight_grads',
            out_shape=[sds((Q, D), BF), sds((C, D), BF), sds((D, FL), BF), sds((FL, D), BF), sds((3, nh, head), F32),
                       sds((S // TP, D), BF), sds((S // TP, D), BF)] + [vshape] * 7,
            in_specs=[any_spec] * 11,
            out_specs=[any_spec] * 4 + [vspec] * 10,
            scratch_shapes=[
                vm((S, D), BF), vm((S, D), BF), vm((S, FL), BF), vm((S, D), BF), vm((Q, S), BF), vm((C, S), BF), vm((D, S), BF),
                vm((FL, S), BF), vm((8, D), F32), vm((S // TP, D), BF), vm((S // TP, D), BF), vm((4, 320, D), BF),
                pltpu.SemaphoreType.DMA((11,)), pltpu.SemaphoreType.DMA((4,)),
            ],
            compiler_params=pltpu.CompilerParams(vmem_limit_bytes=60 * 1024 * 1024),
        )(h, ga, dpre, gyf, dqkv, ctx, gt, rt, vec, y, gx)
        dwqkv, dwout, dwup, dwdn, dbqkv, y, gx, g_ln1g, g_ln1b, g_ln2g, g_ln2b, g_bout, g_bdown, g_bup = outs
        dwqkv = jnp.transpose(dwqkv.reshape(nh, 3, head, D), (3, 0, 1, 2))
        dbqkv = jnp.transpose(dbqkv, (1, 0, 2))
        return (y.reshape(x.shape), gx.reshape(x.shape), g_ln1g, g_ln1b, dwqkv, dbqkv, dwout, g_bout,
                g_ln2g, g_ln2b, dwup, g_bup, dwdn, g_bdown)

    row_spec = P('dp', 'tp', None)
    in_specs = (row_spec, P(), P(), P(None, 'tp', None, None), P('tp', None, None), P('tp', None), P(), P(), P(),
                P(None, 'tp'), P('tp'), P('tp', None), P(), row_spec)
    out_specs = (row_spec, row_spec, P('dp'), P('dp'), P('dp', 'tp', None, None), P(('dp', 'tp'), None, None),
                 P(('dp', 'tp'), None), P('dp'), P('dp'), P('dp'), P('dp', 'tp'), P(('dp', 'tp')), P(('dp', 'tp'), None), P('dp'))
    return jax.shard_map(local_step, mesh=mesh, in_specs=in_specs, out_specs=out_specs, check_vma=False)
```

time: 201 us -> 85.4 us (0.42)
  matrix products: 78.2 us -> 0 us
  Pallas kernels: 0 us -> 74.8 us
  blocking collectives: 55.8 us -> 0 us
  other arithmetic: 23 us -> 0 us
  waiting for transfers between devices: 22.2 us -> 0 us
  between operations: 14.1 us -> 0.84 us
  local copies, waits for them, and re-layouts: 6.25 us -> 9.19 us
    pallas_call x0 -> x2, Pallas kernels: none -> 74.8 us  [the longest x1 57.8 us: local_step(): pl.pallas_call(layer_kernel, name='layer', out_shape=[sds((S // TP, D), B...]
    dot_general x15 -> x0, matrix products: 67.8 us -> none  [the longest x1 10.4 us: local_step(): jnp.einsum('bsd,fd->bsf', grad_m_full, w_down, preferred_element_type=jnp...]
    all_gather x4 -> x0, blocking collectives: 43.9 us -> none  [seq_gather(): return lax.all_gather(values, 'tp', axis=1, tiled=True)]
    reduce_scatter x4 -> x0, waiting for transfers between devices: 22.2 us -> none  [seq_reduce(): return lax.psum_scatter(values, 'tp', scatter_dimension=1, tiled=True)]
    reduce_sum x10 -> x0, other arithmetic: 12.5 us -> none  [the longest x4 5.02 us: layer_norm(): return centered * lax.rsqrt(variance + EPS) * ln_gain + ln_bias]
    psum x1 -> x0, blocking collectives: 11.9 us -> none  [local_step(): grad_ln1_gamma = lax.psum(grad_ln1_gamma, 'tp')]
    convert_element_type x8 -> x0, other arithmetic: 9.79 us -> none  [the longest x1 4.64 us: local_step(): jnp.einsum('bsd,bshte->dhte', h_full, grad_qkv, preferred_element_type=jn...]
    reshape x0 -> x7, local copies, waits for them, and re-layouts: none -> 9.19 us  [local_step(): row = lambda v: v.reshape(1, D)]
  transfers between devices with their start and end apart: 4 -> 0, of which waited for: 2 -> 0; matrix products, arithmetic and copies ran while one was open for 20% -> 0% of each run, Pallas kernels for 0% -> 0%
where the time goes in v1:
time: 85.4 us; the launch traced here: 84.8 us
  Pallas kernels  74.8 us (88%)
  local copies, waits for them, and re-layouts  9.19 us (11%)
    pallas_call x1, Pallas kernels, local_step(): pl.pallas_call(layer_kernel, name='layer', out_shape=[sds((S // TP, D), B...  57.8 us
    pallas_call x1, Pallas kernels, local_step(): pl.pallas_call(grad_kernel, name='weight_grads', out_shape=[sds((Q, D), B...  17 us
    reshape x7, local copies, waits for them, and re-layouts, local_step(): row = lambda v: v.reshape(1, D)  9.19 us

profile of v1, /device:TPU:0, one launch (start us, length us, event | category | flops | bytes accessed | tf_op | source)
XLA Modules:
  0.0 84.8 jit_solution(12524130637194064294)
XLA Ops:
  0.6 1.3 %reshape.70.ln1g_h = f32[1,2560]{1,0:T(1,128)} reshape(f32[2560]{0:T(1024)} %param.15) | data formatting | bytes 20480 | tf_op jit(solution)/shard_map/reshape | solution.py:467
  2.0 1.3 %reshape.71.ln1b_h = f32[1,2560]{1,0:T(1,128)} reshape(f32[2560]{0:T(1024)} %param.16) | data formatting | bytes 20480 | tf_op jit(solution)/shard_map/reshape | solution.py:467
  3.3 1.3 %reshape.74.bout_h = f32[1,2560]{1,0:T(1,128)} reshape(f32[2560]{0:T(1024)} %param.20) | data formatting | bytes 20480 | tf_op jit(solution)/shard_map/reshape | solution.py:467
  4.6 1.3 %reshape.72.ln2g_h = f32[1,2560]{1,0:T(1,128)} reshape(f32[2560]{0:T(1024)} %param.21) | data formatting | bytes 20480 | tf_op jit(solution)/shard_map/reshape | solution.py:467
  5.9 1.3 %reshape.73.ln2b_h = f32[1,2560]{1,0:T(1,128)} reshape(f32[2560]{0:T(1024)} %param.22) | data formatting | bytes 20480 | tf_op jit(solution)/shard_map/reshape | solution.py:467
  7.2 1.3 %reshape.76.bup_h = f32[1,2560]{1,0:T(1,128)} reshape(f32[2560]{0:T(1024)} %param.24) | data formatting | bytes 20480 | tf_op jit(solution)/shard_map/reshape | solution.py:467
  8.5 1.3 %reshape.75.bdown_h = f32[1,2560]{1,0:T(1,128)} reshape(f32[2560]{0:T(1024)} %param.26) | data formatting | bytes 20480 | tf_op jit(solution)/shard_map/reshape | solution.py:467
  9.8 57.8 %layer.1 = (bf16[32,2560]{1,0:T(8,128)(2,1)}, bf16[32,2560]{1,0:T(8,128)(2,1)}, f32[8,2560]{1,0:T(8,128)}, bf16[128,2560]{1,0:T(8,128)(2,1)}, bf16[128,2560]{1,0...) custom-call(bf16[32,2560]{1,0:T(8,128)(2,1)} %bitcast.13, ...), custom_call_target="tpu_custom_call" | custom-call | tf_op jit(solution)/shard_map/layer/pallas_call | solution.py:468
  67.6 17.0 %weight_grads.1 = (bf16[1920,2560]{1,0:T(8,128)(2,1)}, bf16[640,2560]{1,0:T(8,128)(2,1)}, bf16[2560,2560]{1,0:T(8,128)(2,1)}, bf16[2560,2560]{1,0:T(8,128)(2,1)}...) custom-call(bf16[128,2560]{1,0:T(8,128)(2,1)} %get-tuple-element.39., ...), custom_call_target="tpu_custom_call" | custom-call | tf_op jit(solution)/shard_map/weight_grads/pallas_call | solution.py:491

commit v2 on v1

--- a/solution.py
+++ b/solution.py
@@ -104,7 +104,7 @@
 
     lx = load(x_h, xg.at[own, :])
     lg = load(gy_h, gyg.at[own, :])
-    lvec = [load(src, vecs.at[k]) for k, src in enumerate((ln1g_h, ln1b_h, ln2g_h, ln2b_h, bout_h, bdown_h, bup_h))]
+    lvec = [load(src, vecs.at[k, 0]) for k, src in enumerate((ln1g_h, ln1b_h, ln2g_h, ln2b_h, bout_h, bdown_h, bup_h))]
     lb = load(bqkv_h, bqkv)
     lwqkv = load(wqkv_h, wqkv)
     lwout = load(wout_h, wout)
@@ -464,7 +464,7 @@
         n_remote = 64
         red = [vm((S, D), BF), vm((S // 2, D), BF), vm((S // 2, D), BF), vm((S // 2, D), BF), vm((S, D), BF)]
         scat = [vm((S, D), BF), vm((S // 2, D), BF), vm((S // 2, D), BF), vm((S // TP, D), BF)]
-        row = lambda v: v.reshape(1, D)
+        row = lambda v: v
         res = pl.pallas_call(
             layer_kernel,
             name='layer',

time: 85.4 us -> 75.8 us (0.89)
  local copies, waits for them, and re-layouts: 9.19 us -> 0 us
    reshape x7 -> x0, local copies, waits for them, and re-layouts: 9.19 us -> none  [local_step(): row = lambda v: v.reshape(1, D)]
where the time goes in v2:
time: 75.8 us; the launch traced here: 75.7 us
  Pallas kernels  74.9 us (99%)
  between operations  0.84 us (1%)
    pallas_call x1, Pallas kernels, local_step(): pl.pallas_call(layer_kernel, name='layer', out_shape=[sds((S // TP, D), B...  57.9 us
    pallas_call x1, Pallas kernels, local_step(): pl.pallas_call(grad_kernel, name='weight_grads', out_shape=[sds((Q, D), B...  17 us

profile of v2, /device:TPU:0, one launch (start us, length us, event | category | flops | bytes accessed | tf_op | source)
XLA Modules:
  0.0 75.7 jit_solution(17024438937210019548)
XLA Ops:
  0.7 57.9 %layer.1 = (bf16[32,2560]{1,0:T(8,128)(2,1)}, bf16[32,2560]{1,0:T(8,128)(2,1)}, f32[8,2560]{1,0:T(8,128)}, bf16[128,2560]{1,0:T(8,128)(2,1)}, bf16[128,2560]{1,0...) custom-call(bf16[32,2560]{1,0:T(8,128)(2,1)} %bitcast.13, ...), custom_call_target="tpu_custom_call" | custom-call | tf_op jit(solution)/shard_map/layer/pallas_call | solution.py:468
  58.5 17.0 %weight_grads.1 = (bf16[1920,2560]{1,0:T(8,128)(2,1)}, bf16[640,2560]{1,0:T(8,128)(2,1)}, bf16[2560,2560]{1,0:T(8,128)(2,1)}, bf16[2560,2560]{1,0:T(8,128)(2,1)}...) custom-call(bf16[128,2560]{1,0:T(8,128)(2,1)} %get-tuple-element.39., ...), custom_call_target="tpu_custom_call" | custom-call | tf_op jit(solution)/shard_map/weight_grads/pallas_call | solution.py:491

commit v3 on v2

v3 whole, which is shorter than its diff:
```python
import functools
import math
import jax
import jax.numpy as jnp
from jax import lax
from jax.experimental import pallas as pl
from jax.experimental.pallas import tpu as pltpu
from jax.sharding import PartitionSpec as P

EPS = 1e-5
MASK_VALUE = -1e30
BF = jnp.bfloat16
F32 = jnp.float32
MESH = pl.DeviceIdType.MESH
GELU_C = math.sqrt(2.0 / math.pi)
GELU_A = 0.044715
TP = 4
LANES = 128
ALL_CHUNKS = (2, 4, 4, 5, 4, 1)
SCATTER_CHUNKS = (2, 4, 5, 5, 4)
N_BLK = 5
N_REMOTE = 61
N_STORE = 12


def alibi_slopes(n_heads):
    closest = 2 ** int(math.floor(math.log2(n_heads)))
    base_ratio = 2.0 ** (-8.0 / closest)
    extra_ratio = 2.0 ** (-4.0 / closest)
    remaining = min(closest, n_heads - closest)
    slopes = [base_ratio ** (i + 1) for i in range(closest)]
    return slopes + [extra_ratio ** (2 * i + 1) for i in range(remaining)]


def dot(lhs, rhs):
    return lax.dot_general(lhs, rhs, (((1,), (0,)), ((), ())), preferred_element_type=F32)


def dot_t(lhs, rhs):
    return lax.dot_general(lhs, rhs, (((1,), (1,)), ((), ())), preferred_element_type=F32)


def layer_kernel(x_h, gy_h, wqkv_h, bqkv_h, wout_h, wup_h, wdn_h, ln1g_h, ln1b_h, ln2g_h, ln2b_h, bout_h, bdown_h, bup_h,
                 y_o, gx_o, vec_o, part_o, h_o, ga_o, dpre_o, gy_o, dqkv_o, ctx_o, gt_o, rt_o,
                 wqkv, wout, wup, wdn, bqkv, vecs, xg, gyg, h, bias, qkv, prob, probb, ctx, x1, xhat, g, gt, rt, gact, r, dpre,
                 gmid, ga, dctx, dqkv, ybuf, gxbuf, xh1, vec, part, ubuf, xr, vt, dpb, dsb,
                 p1, rd1, s1, rs1, t1, q1, e1, p2, rd2, s2, rs2, t2, q2, e2, py, rdy, sy, rsy, ph, rdh, sh, rsh,
                 lsem, osem, ssem, rsem):
    D = x_h.shape[1]
    seq = TP * 32
    head = bqkv_h.shape[2]
    n_heads = bqkv_h.shape[1]
    nlc = D // LANES
    t = lax.axis_index('tp')
    core = lax.rem(t, 2)
    chip = t // 2
    sib = t + 1 - 2 * core
    cross = lax.rem(t + 2, TP)
    sibcross = lax.rem(sib + 2, TP)

    def slot(dev):
        return lax.rem(dev, 2) * 2 + dev // 2

    def rows(dev):
        return pl.ds(pl.multiple_of(slot(dev) * 32, 32), 32)

    own = rows(t)
    half = pl.ds(pl.multiple_of(core * 64, 64), 64)
    sibhalf = pl.ds(pl.multiple_of((1 - core) * 64, 64), 64)
    blk_own = pl.ds(pl.multiple_of(chip * 32, 32), 32)
    blk_cross = pl.ds(pl.multiple_of((1 - chip) * 32, 32), 32)

    counter = [0, 0, 0]

    def load(src, dst):
        k = counter[0]
        counter[0] += 1
        copy = pltpu.make_async_copy(src, dst, lsem.at[k])
        copy.start()
        return copy

    outs = []

    def store(src, dst):
        k = counter[1]
        counter[1] += 1
        copy = pltpu.make_async_copy(src, dst, osem.at[k])
        copy.start()
        outs.append(copy)

    sent = []

    def remote(src, dst, dev):
        k = counter[2]
        counter[2] += 1
        copy = pltpu.make_async_remote_copy(src_ref=src, dst_ref=dst, send_sem=ssem.at[k], recv_sem=rsem.at[k],
                                            device_id={'tp': dev}, device_id_type=MESH)
        copy.start()
        sent.append(copy)
        return copy

    def lc(c):
        return slice(c * LANES, (c + 1) * LANES)

    def groups(widths, j):
        start = sum(widths[:j])
        return range(start, start + widths[j])

    def cols(widths, j):
        return slice(sum(widths[:j]) * LANES, sum(widths[:j + 1]) * LANES)

    lx = load(x_h, xg.at[own, :])
    lg = load(gy_h, gyg.at[own, :])
    lvec = [load(src, vecs.at[k, 0]) for k, src in enumerate((ln1g_h, ln1b_h, ln2g_h, ln2b_h, bout_h, bdown_h, bup_h))]
    lb = load(bqkv_h, bqkv)
    lwqkv = load(wqkv_h, wqkv)
    lwout = load(wout_h, wout)
    barrier = pltpu.get_barrier_semaphore()
    for dev in (sib, cross, sibcross):
        pl.semaphore_signal(barrier, inc=1, device_id={'tp': dev}, device_id_type=MESH)
    pl.semaphore_wait(barrier, 3)
    lx.wait()
    def piece(dev, k):
        return pl.ds(pl.multiple_of(slot(dev) * 32 + 16 * k, 16), 16)

    x_to_cross = [remote(xg.at[piece(t, k), :], xg.at[piece(t, k), :], cross) for k in range(2)]
    x_to_sib = remote(xg.at[own, :], xg.at[own, :], sib)
    lg.wait()
    gy_to_sib = remote(gyg.at[own, :], gyg.at[own, :], sib)
    lwdn = load(wdn_h, wdn)
    lwup = load(wup_h, wup)
    for copy in lvec:
        copy.wait()

    def ln_block(rr, n, src, gain, shift, dst):
        acc = jnp.zeros((n, LANES), F32)
        for c in range(nlc):
            acc = acc + src[rr, lc(c)].astype(F32)
        mean = jnp.sum(acc, axis=1, keepdims=True) / D
        acc = jnp.zeros((n, LANES), F32)
        for c in range(nlc):
            z = src[rr, lc(c)].astype(F32) - mean
            acc = acc + z * z
        rstd = lax.rsqrt(jnp.sum(acc, axis=1, keepdims=True) / D + EPS)
        for c in range(nlc):
            z = (src[rr, lc(c)].astype(F32) - mean) * rstd
            if dst is not None:
                dst[rr, lc(c)] = (z * vecs[gain, :, lc(c)] + vecs[shift, :, lc(c)]).astype(BF)
            else:
                xh1[:, lc(c)] = z
        return rstd

    ln_block(own, 32, xg, 0, 1, h)
    lb.wait()
    for k in range(3):
        bt = bqkv[k].T
        for hd in range(n_heads):
            at = (hd * 3 + k) * head
            bias[at:at + head, :] = jnp.broadcast_to(bt[:head, hd:hd + 1], (head, seq))
    x_to_sib.wait_recv()
    ln_block(rows(sib), 32, xg, 0, 1, h)
    x_fwd = []
    for k in range(2):
        x_to_cross[k].wait_recv()
        x_fwd.append(remote(xg.at[piece(cross, k), :], xg.at[piece(cross, k), :], sib))
    gy_to_cross = remote(gyg.at[own, :], gyg.at[own, :], cross)
    lwqkv.wait()
    lwout.wait()
    ln_block(rows(cross), 32, xg, 0, 1, h)
    for k in range(2):
        x_fwd[k].wait_recv()
    ln_block(rows(sibcross), 32, xg, 0, 1, h)

    hr = 2 * 3 * head
    hv = h[...]
    for m in range(n_heads // 2):
        mm = slice(m * hr, (m + 1) * hr)
        qkv[mm, :] = (dot_t(wqkv[mm, :], hv) + bias[mm, :]).astype(BF)

    def position(axis):
        i = lax.broadcasted_iota(jnp.int32, (seq, seq), axis)
        b = i >> 5
        return ((((b & 1) << 1) | (b >> 1)) << 5) | (i & 31)

    pos_k = position(0)
    causal = pos_k <= position(1)
    key_f = pos_k.astype(F32)
    slopes = alibi_slopes(n_heads * TP)
    score_scale = head ** -0.5

    def part_of(hd, k):
        at = (hd * 3 + k) * head
        return slice(at, at + head)

    def slope(hd):
        v = jnp.float32(slopes[hd])
        for dev in range(1, TP):
            v = jnp.where(t == dev, jnp.float32(slopes[dev * n_heads + hd]), v)
        return v

    for hd in range(n_heads):
        s = dot(qkv[part_of(hd, 1), :].T, qkv[part_of(hd, 0), :]) * score_scale + slope(hd) * key_f
        s = jnp.where(causal, s, MASK_VALUE)
        e = jnp.exp(s - jnp.max(s, axis=0, keepdims=True))
        pr = e * (1.0 / jnp.sum(e, axis=0, keepdims=True))
        prob[hd] = pr
        probb[hd] = pr.astype(BF)
    for hd in range(n_heads):
        ctx[hd * head:(hd + 1) * head, :] = dot(qkv[part_of(hd, 2), :], probb[hd]).astype(BF)

    class AllSum:
        widths = ALL_CHUNKS

        def __init__(self, p, rd, s, rs, tt, q, e):
            self.p, self.rd, self.s, self.rs, self.tt, self.q, self.e = p, rd, s, rs, tt, q, e
            self.a, self.b, self.c = {}, {}, {}
            self.last = len(self.widths) - 1

        def ch(self, j):
            return cols(self.widths, j)

        def fill(self, j, value):
            self.p[:, self.ch(j)] = value

        def put(self, j):
            self.a[j] = remote(self.p.at[sibhalf, self.ch(j)], self.rd.at[:, self.ch(j)], sib)

        def pair(self, j):
            self.a[j].wait_recv()
            c = self.ch(j)
            self.s[:, c] = (self.p[half, c].astype(F32) + self.rd[:, c].astype(F32)).astype(BF)

        def step_cross(self, j):
            self.pair(j)
            c = self.ch(j)
            self.b[j] = remote(self.s.at[:, c], self.rs.at[:, c], cross)
            if j == self.last:
                self.c[j] = (remote(self.s.at[:, c], self.e.at[:, :], sibcross), remote(self.s.at[:, c], self.q.at[:, :], sib))

        def step_back(self, j):
            self.b[j].wait_recv()
            c = self.ch(j)
            self.tt[half, c] = (self.s[:, c].astype(F32) + self.rs[:, c].astype(F32)).astype(BF)
            if j < self.last:
                self.c[j] = remote(self.tt.at[half, c], self.tt.at[half, c], sib)

        def finish(self, j):
            if j < self.last:
                self.c[j].wait_recv()
            else:
                for copy in self.c[j]:
                    copy.wait_recv()
                self.tt[sibhalf, self.ch(j)] = (self.q[...].astype(F32) + self.e[...].astype(F32)).astype(BF)

    class ScatterSum(AllSum):
        widths = SCATTER_CHUNKS

        def step_cross(self, j):
            self.pair(j)
            c = self.ch(j)
            self.b[j] = remote(self.s.at[blk_cross, c], self.rs.at[:, c], cross)

        def result(self, c):
            return (self.s[blk_own, c].astype(F32) + self.rs[:, c].astype(F32)).astype(BF).astype(F32)

    o_flat = ctx[...].T
    sum_a = AllSum(p1, rd1, s1, rs1, t1, q1, e1)
    n_all = len(ALL_CHUNKS)
    sum_a.fill(0, dot(o_flat, wout[:, sum_a.ch(0)]).astype(BF))
    sum_a.put(0)
    for j in range(1, n_all):
        sum_a.fill(j, dot(o_flat, wout[:, sum_a.ch(j)]).astype(BF))
    for j in range(1, n_all):
        sum_a.put(j)
    for j in range(n_all):
        sum_a.step_cross(j)
    store(h, h_o)
    store(ctx, ctx_o)

    gy_to_sib.wait_recv()
    gy_to_cross.wait_recv()
    gy_fwd = remote(gyg.at[rows(cross), :], gyg.at[rows(cross), :], sib)
    for hd in range(n_heads):
        vt[hd] = qkv[part_of(hd, 2), :].T
    gy_fwd.wait_recv()
    store(gyg, gy_o)
    lwdn.wait()
    lwup.wait()
    fw = wdn_h.shape[0] // N_BLK
    acc = jnp.zeros((seq, LANES), F32)

    def x1_chunk(j, acc):
        sum_a.finish(j)
        for c in groups(ALL_CHUNKS, j):
            z = xg[:, lc(c)].astype(F32) + t1[:, lc(c)].astype(F32) + vecs[4, :, lc(c)]
            x1[:, lc(c)] = z
            acc = acc + z
        return acc

    gyv = gyg[...]
    for j in range(n_all):
        if j < N_BLK:
            ff = slice(j * fw, (j + 1) * fw)
            gact[:, ff] = dot_t(gyv, wdn[ff, :]).astype(BF)
        sum_a.step_back(j)
        if j:
            acc = x1_chunk(j - 1, acc)
    acc = x1_chunk(n_all - 1, acc)

    mean = jnp.sum(acc, axis=1, keepdims=True) / D
    halves = (slice(0, seq // 2), slice(seq // 2, seq))
    rstd2 = []
    for n, hh in enumerate(halves):
        acc = jnp.zeros((seq // 2, LANES), F32)
        for c in range(nlc):
            z = x1[hh, lc(c)] - mean[hh]
            acc = acc + z * z
        rstd2.append(lax.rsqrt(jnp.sum(acc, axis=1, keepdims=True) / D + EPS))
    for n, hh in enumerate(halves):
        for c in range(nlc):
            z = (x1[hh, lc(c)] - mean[hh]) * rstd2[n]
            xhat[hh, lc(c)] = z
            g[hh, lc(c)] = (z * vecs[2, :, lc(c)] + vecs[3, :, lc(c)]).astype(BF)

    gv = g[...]
    for j in range(N_BLK):
        ff = slice(j * fw, (j + 1) * fw)
        pre = dot(gv, wup[:, ff]) + vecs[6, :, ff]
        w = (GELU_C * GELU_A) * (pre * pre)
        th = jnp.tanh(pre * (GELU_C + w))
        hp = 0.5 * pre
        r[:, ff] = (hp + hp * th).astype(BF)
        slope_g = (0.5 + 0.5 * th) + (hp * (1.0 - th * th)) * (GELU_C + 3.0 * w)
        gp = gact[:, ff].astype(F32) * slope_g
        vec[6:7, ff] = jnp.sum(gp, axis=0, keepdims=True)
        dpre[:, ff] = gp.astype(BF)

    dv = dpre[...]
    sum_g = AllSum(p2, rd2, s2, rs2, t2, q2, e2)
    for j in range(n_all):
        sum_g.fill(j, dot_t(dv, wup[sum_g.ch(j), :]).astype(BF))
        sum_g.put(j)
        if j:
            sum_g.step_cross(j - 1)
    sum_g.step_cross(n_all - 1)
    store(dpre, dpre_o)

    acc1 = jnp.zeros((seq, LANES), F32)
    acc2 = jnp.zeros((seq, LANES), F32)

    def ln2_back_chunk(j, acc1, acc2):
        sum_g.finish(j)
        for c in groups(ALL_CHUNKS, j):
            dg = t2[:, lc(c)].astype(F32)
            z = xhat[:, lc(c)]
            dgz = dg * z
            vec[2:3, lc(c)] = jnp.sum(dgz, axis=0, keepdims=True)
            vec[3:4, lc(c)] = jnp.sum(dg, axis=0, keepdims=True)
            gain = vecs[2, :, lc(c)]
            dz = dg * gain
            acc1 = acc1 + dz
            acc2 = acc2 + dgz * gain
            for n, hh in enumerate(halves):
                ubuf[hh, lc(c)] = gyg[hh, lc(c)].astype(F32) + rstd2[n] * dz[hh]
        return acc1, acc2

    rv = r[...]
    yw = D // N_BLK
    for j in range(n_all):
        if j < N_BLK:
            yy = slice(j * yw, (j + 1) * yw)
            py[:, yy] = dot(rv, wdn[:, yy]).astype(BF)
            for c in range(j * (yw // LANES), (j + 1) * (yw // LANES)):
                gt[lc(c), :] = g[:, lc(c)].T
                rt[lc(c), :] = r[:, lc(c)].T
                vec[5:6, lc(c)] = jnp.sum(gyg[:, lc(c)].astype(F32), axis=0, keepdims=True)
                for n, hh in enumerate(halves):
                    xr[hh, lc(c)] = xhat[hh, lc(c)] * rstd2[n]
        if j == N_BLK:
            y_sib = remote(py.at[sibhalf, :], rdy, sib)
            store(gt, gt_o)
            store(rt, rt_o)
        sum_g.step_back(j)
        if j:
            acc1, acc2 = ln2_back_chunk(j - 1, acc1, acc2)
    y_sib.wait_recv()
    sy[...] = (py[half, :].astype(F32) + rdy[...].astype(F32)).astype(BF)
    y_cross = remote(sy.at[blk_cross, :], rsy, cross)
    acc1, acc2 = ln2_back_chunk(n_all - 1, acc1, acc2)

    for n, hh in enumerate(halves):
        mean1 = rstd2[n] * (jnp.sum(acc1[hh], axis=1, keepdims=True) / D)
        mean2 = jnp.sum(acc2[hh], axis=1, keepdims=True) / D
        for c in range(nlc):
            gm = ubuf[hh, lc(c)] - (mean1 + xr[hh, lc(c)] * mean2)
            gmid[hh, lc(c)] = gm
            ga[hh, lc(c)] = gm.astype(BF)

    gav = ga[...]
    hc = ctx.shape[0] // 2
    for k in range(2):
        dctx[k * hc:(k + 1) * hc, :] = dot_t(wout[k * hc:(k + 1) * hc, :], gav).astype(BF)

    def head_rows(hd):
        return slice(hd * head, (hd + 1) * head)

    for hd in range(n_heads):
        dpb[hd] = dot(vt[hd], dctx[head_rows(hd), :]).astype(BF)
    for hd in range(n_heads):
        dqkv[part_of(hd, 2), :] = dot_t(dctx[head_rows(hd), :], probb[hd]).astype(BF)
    for hd in range(n_heads):
        pr = prob[hd]
        dp = dpb[hd].astype(F32)
        dsb[hd] = (pr * (dp - jnp.sum(dp * pr, axis=0, keepdims=True))).astype(BF)
    for hd in range(n_heads):
        dqkv[part_of(hd, 0), :] = (dot(qkv[part_of(hd, 1), :], dsb[hd]) * score_scale).astype(BF)
        dqkv[part_of(hd, 1), :] = (dot_t(qkv[part_of(hd, 0), :], dsb[hd]) * score_scale).astype(BF)

    sum_h = ScatterSum(ph, rdh, sh, rsh, None, None, None)
    n_scat = len(SCATTER_CHUNKS)
    dq = dqkv[...].T
    for j in range(n_scat):
        sum_h.fill(j, dot(dq, wqkv[:, sum_h.ch(j)]).astype(BF))
        sum_h.put(j)
        if j:
            sum_h.step_cross(j - 1)
    sum_h.step_cross(n_scat - 1)
    store(ga, ga_o)
    store(dqkv, dqkv_o)

    rstd1 = ln_block(own, 32, xg, 0, 1, None)
    y_cross.wait_recv()
    for c in range(nlc):
        z = (sy[blk_own, lc(c)].astype(F32) + rsy[:, lc(c)].astype(F32)).astype(BF).astype(F32)
        ybuf[:, lc(c)] = (x1[own, lc(c)] + z + vecs[5, :, lc(c)]).astype(BF)
        vec[4:5, lc(c)] = jnp.sum(gmid[:, lc(c)], axis=0, keepdims=True)
    store(ybuf, y_o)
    store(vec, vec_o)

    me = slot(t)
    acc1 = jnp.zeros((32, LANES), F32)
    acc2 = jnp.zeros((32, LANES), F32)
    for j in range(n_scat):
        sum_h.b[j].wait_recv()
        for c in groups(SCATTER_CHUNKS, j):
            dh = sum_h.result(lc(c))
            z = xh1[:, lc(c)]
            dhz = dh * z
            part[0:1, lc(c)] = jnp.sum(dhz, axis=0, keepdims=True)
            part[1:2, lc(c)] = jnp.sum(dh, axis=0, keepdims=True)
            gain = vecs[0, :, lc(c)]
            acc1 = acc1 + dh * gain
            acc2 = acc2 + dhz * gain
    parts = [remote(part, part_o.at[me], dev) for dev in (cross, sibcross, sib)]
    store(part, part_o.at[me])
    mean1 = jnp.sum(acc1, axis=1, keepdims=True) / D
    mean2 = jnp.sum(acc2, axis=1, keepdims=True) / D
    for c in range(nlc):
        dz = sum_h.result(lc(c)) * vecs[0, :, lc(c)]
        gxbuf[:, lc(c)] = (gmid[own, lc(c)] + rstd1 * (dz - mean1 - xh1[:, lc(c)] * mean2)).astype(BF)
    store(gxbuf, gx_o)
    for copy in sent:
        copy.wait_send()
    for copy in outs:
        copy.wait()
    for copy in parts:
        copy.wait_recv()


def grad_kernel(h_h, ga_h, dpre_h, gy_h, dqkv_h, ctx_h, gt_h, rt_h, vec_h, part_h, y_h, gx_h,
                dwqkv_o, dwout_o, dwup_o, dwdn_o, dbqkv_o, y_o, gx_o, v0, v1, v2, v3, v4, v5, v6,
                h, ga, dpre, gy, dqkv, ctx, gt, rt, vec, part, y, gx, buf, isem, osem):
    n_heads, head = dbqkv_o.shape[1], dbqkv_o.shape[2]
    block = 320
    slots = buf.shape[0]
    pairs = ((rt_h, rt), (gy_h, gy), (gt_h, gt), (dpre_h, dpre), (dqkv_h, dqkv), (h_h, h), (ctx_h, ctx), (ga_h, ga), (vec_h, vec),
             (part_h, part), (y_h, y), (gx_h, gx))
    loads = []

    def fetch(n):
        for src, dst in pairs[len(loads):n]:
            copy = pltpu.make_async_copy(src, dst, isem.at[len(loads)])
            copy.start()
            loads.append(copy)

    fetch(2)
    step = 0
    pending = []
    for n, (left, right, out) in enumerate(((rt, gy, dwdn_o), (gt, dpre, dwup_o), (dqkv, h, dwqkv_o), (ctx, ga, dwout_o))):
        loads[2 * n].wait()
        loads[2 * n + 1].wait()
        if n == 0:
            fetch(len(pairs))
        rv = right[...]
        for m in range(left.shape[0] // block):
            s = step % slots
            if step >= slots:
                pending[step - slots].wait()
            mm = slice(m * block, (m + 1) * block)
            buf[s] = dot(left[mm, :], rv).astype(BF)
            copy = pltpu.make_async_copy(buf.at[s], out.at[pl.ds(m * block, block), :], osem.at[s])
            copy.start()
            pending.append(copy)
            step += 1
    ones = jnp.ones((8, dqkv.shape[1]), BF)
    sums = dot_t(ones, dqkv[...])[0:1]
    for k in range(3):
        for hd in range(n_heads):
            at = (hd * 3 + k) * head
            dbqkv_o[k, hd:hd + 1, :] = sums[:, at:at + head]
    for k in range(8, 12):
        loads[k].wait()
    y_o[...] = y[...]
    gx_o[...] = gx[...]
    for k, o in enumerate((v0, v1)):
        o[...] = (part[0, k, :] + part[1, k, :]) + (part[2, k, :] + part[3, k, :])
    for k, o in enumerate((v2, v3, v4, v5, v6)):
        o[...] = vec[2 + k, :]
    for k in range(max(0, step - slots), step):
        pending[k].wait()


def solution(mesh):
    def local_step(x, ln1_gamma, ln1_beta, w_qkv, b_qkv, w_out, b_out, ln2_gamma, ln2_beta, w_up, b_up, w_down, b_down, grad_y):
        D = x.shape[2]
        S = TP * x.shape[1]
        nh, head = w_qkv.shape[1], w_qkv.shape[3]
        Q = nh * 3 * head
        C = nh * head
        FL = w_up.shape[1]
        any_spec = pl.BlockSpec(memory_space=pl.ANY)
        vm = pltpu.VMEM
        wqkv_t = jnp.transpose(w_qkv, (1, 2, 3, 0)).reshape(Q, D)
        bq = jnp.transpose(b_qkv, (1, 0, 2))
        sds = jax.ShapeDtypeStruct
        n_loads = 2 + 7 + 1 + 4
        red = [vm((S, D), BF), vm((S // 2, D), BF), vm((S // 2, D), BF), vm((S // 2, D), BF), vm((S, D), BF),
               vm((S // 2, ALL_CHUNKS[-1] * LANES), BF), vm((S // 2, ALL_CHUNKS[-1] * LANES), BF)]
        scat = [vm((S, D), BF), vm((S // 2, D), BF), vm((S // 2, D), BF), vm((S // TP, D), BF)]
        row = lambda v: v
        res = pl.pallas_call(
            layer_kernel,
            name='layer',
            out_shape=[sds((S // TP, D), BF), sds((S // TP, D), BF), sds((8, D), F32), sds((TP, 2, D), F32), sds((S, D), BF), sds((S, D), BF),
                       sds((S, FL), BF), sds((S, D), BF), sds((Q, S), BF), sds((C, S), BF), sds((D, S), BF), sds((FL, S), BF)],
            in_specs=[any_spec] * 14,
            out_specs=[any_spec] * 12,
            scratch_shapes=[
                vm((Q, D), BF), vm((C, D), BF), vm((D, FL), BF), vm((FL, D), BF), vm((3, nh, head), F32), vm((7, 1, D), F32),
                vm((S, D), BF), vm((S, D), BF), vm((S, D), BF), vm((Q, S), F32), vm((Q, S), BF), vm((nh, S, S), F32),
                vm((nh, S, S), BF), vm((C, S), BF), vm((S, D), F32), vm((S, D), F32), vm((S, D), BF), vm((D, S), BF), vm((FL, S), BF),
                vm((S, FL), BF), vm((S, FL), BF), vm((S, FL), BF), vm((S, D), F32), vm((S, D), BF), vm((C, S), BF), vm((Q, S), BF),
                vm((S // TP, D), BF), vm((S // TP, D), BF), vm((S // TP, D), F32), vm((8, D), F32), vm((2, D), F32), vm((S, D), F32), vm((S, D), F32),
                vm((nh, S, head), BF), vm((nh, S, S), BF), vm((nh, S, S), BF),
                *red, *red, *scat, *scat,
                pltpu.SemaphoreType.DMA((n_loads,)), pltpu.SemaphoreType.DMA((N_STORE,)),
                pltpu.SemaphoreType.DMA((N_REMOTE,)), pltpu.SemaphoreType.DMA((N_REMOTE,)),
            ],
            compiler_params=pltpu.CompilerParams(collective_id=0, has_side_effects=True, vmem_limit_bytes=67043328),
        )(x.reshape(x.shape[1], D), grad_y.reshape(x.shape[1], D), wqkv_t, bq, w_out, w_up, w_down, row(ln1_gamma), row(ln1_beta),
          row(ln2_gamma), row(ln2_beta), row(b_out), row(b_down), row(b_up))
        y, gx, vec, part, h, ga, dpre, gyf, dqkv, ctx, gt, rt = res
        vspec = pl.BlockSpec(memory_space=pltpu.VMEM)
        vshape = sds((D,), F32)
        outs = pl.pallas_call(
            grad_kernel,
            name='weight_grads',
            out_shape=[sds((Q, D), BF), sds((C, D), BF), sds((D, FL), BF), sds((FL, D), BF), sds((3, nh, head), F32),
                       sds((S // TP, D), BF), sds((S // TP, D), BF)] + [vshape] * 7,
            in_specs=[any_spec] * 12,
            out_specs=[any_spec] * 4 + [vspec] * 10,
            scratch_shapes=[
                vm((S, D), BF), vm((S, D), BF), vm((S, FL), BF), vm((S, D), BF), vm((Q, S), BF), vm((C, S), BF), vm((D, S), BF),
                vm((FL, S), BF), vm((8, D), F32), vm((TP, 2, D), F32), vm((S // TP, D), BF), vm((S // TP, D), BF), vm((4, 320, D), BF),
                pltpu.SemaphoreType.DMA((12,)), pltpu.SemaphoreType.DMA((4,)),
            ],
            compiler_params=pltpu.CompilerParams(vmem_limit_bytes=60 * 1024 * 1024),
        )(h, ga, dpre, gyf, dqkv, ctx, gt, rt, vec, part, y, gx)
        dwqkv, dwout, dwup, dwdn, dbqkv, y, gx, g_ln1g, g_ln1b, g_ln2g, g_ln2b, g_bout, g_bdown, g_bup = outs
        dwqkv = jnp.transpose(dwqkv.reshape(nh, 3, head, D), (3, 0, 1, 2))
        dbqkv = jnp.transpose(dbqkv, (1, 0, 2))
        return (y.reshape(x.shape), gx.reshape(x.shape), g_ln1g, g_ln1b, dwqkv, dbqkv, dwout, g_bout,
                g_ln2g, g_ln2b, dwup, g_bup, dwdn, g_bdown)

    row_spec = P('dp', 'tp', None)
    in_specs = (row_spec, P(), P(), P(None, 'tp', None, None), P('tp', None, None), P('tp', None), P(), P(), P(),
                P(None, 'tp'), P('tp'), P('tp', None), P(), row_spec)
    out_specs = (row_spec, row_spec, P('dp'), P('dp'), P('dp', 'tp', None, None), P(('dp', 'tp'), None, None),
                 P(('dp', 'tp'), None), P('dp'), P('dp'), P('dp'), P('dp', 'tp'), P(('dp', 'tp')), P(('dp', 'tp'), None), P('dp'))
    return jax.shard_map(local_step, mesh=mesh, in_specs=in_specs, out_specs=out_specs, check_vma=False)
```

time: 75.8 us -> 71.4 us (0.942)
  Pallas kernels: 74.9 us -> 70.5 us
    pallas_call x1, Pallas kernels: 57.9 us -> 53.5 us  [local_step(): pl.pallas_call(layer_kernel, name='layer', out_shape=[sds((S // TP, D), B...]
where the time goes in v3:
time: 71.4 us; the launch traced here: 71.3 us
  Pallas kernels  70.5 us (99%)
  between operations  0.84 us (1%)
    pallas_call x1, Pallas kernels, local_step(): pl.pallas_call(layer_kernel, name='layer', out_shape=[sds((S // TP, D), B...  53.5 us
    pallas_call x1, Pallas kernels, local_step(): pl.pallas_call(grad_kernel, name='weight_grads', out_shape=[sds((Q, D), B...  17 us

profile of v3, /device:TPU:0, one launch (start us, length us, event | category | flops | bytes accessed | tf_op | source)
XLA Modules:
  0.0 71.3 jit_solution(4025269384336818353)
XLA Ops:
  0.7 53.5 %layer.1 = (bf16[32,2560]{1,0:T(8,128)(2,1)}, bf16[32,2560]{1,0:T(8,128)(2,1)}, f32[8,2560]{1,0:T(8,128)}, f32[4,2,2560]{2,1,0:T(2,128)}, bf16[128,2560]{1,0:T(8...) custom-call(bf16[32,2560]{1,0:T(8,128)(2,1)} %bitcast.13, ...), custom_call_target="tpu_custom_call" | custom-call | tf_op jit(solution)/shard_map/layer/pallas_call | solution.py:541
  54.1 17.0 %weight_grads.1 = (bf16[1920,2560]{1,0:T(8,128)(2,1)}, bf16[640,2560]{1,0:T(8,128)(2,1)}, bf16[2560,2560]{1,0:T(8,128)(2,1)}, bf16[2560,2560]{1,0:T(8,128)(2,1)}...) custom-call(bf16[128,2560]{1,0:T(8,128)(2,1)} %get-tuple-element.40., ...), custom_call_target="tpu_custom_call" | custom-call | tf_op jit(solution)/shard_map/weight_grads/pallas_call | solution.py:565

commit v4 on v3

--- a/solution.py
+++ b/solution.py
@@ -17,9 +17,9 @@
 TP = 4
 LANES = 128
 ALL_CHUNKS = (2, 4, 4, 5, 4, 1)
-SCATTER_CHUNKS = (2, 4, 5, 5, 4)
+SCATTER_CHUNKS = (6, 6, 5, 3)
 N_BLK = 5
-N_REMOTE = 61
+N_REMOTE = 59
 N_STORE = 12
 
 
@@ -199,8 +199,9 @@
         return v
 
     for hd in range(n_heads):
-        s = dot(qkv[part_of(hd, 1), :].T, qkv[part_of(hd, 0), :]) * score_scale + slope(hd) * key_f
-        s = jnp.where(causal, s, MASK_VALUE)
+        prob[hd] = dot(qkv[part_of(hd, 1), :].T, qkv[part_of(hd, 0), :])
+    for hd in range(n_heads):
+        s = jnp.where(causal, prob[hd] * score_scale + slope(hd) * key_f, MASK_VALUE)
         e = jnp.exp(s - jnp.max(s, axis=0, keepdims=True))
         pr = e * (1.0 / jnp.sum(e, axis=0, keepdims=True))
         prob[hd] = pr
@@ -469,11 +470,10 @@
 
 def grad_kernel(h_h, ga_h, dpre_h, gy_h, dqkv_h, ctx_h, gt_h, rt_h, vec_h, part_h, y_h, gx_h,
                 dwqkv_o, dwout_o, dwup_o, dwdn_o, dbqkv_o, y_o, gx_o, v0, v1, v2, v3, v4, v5, v6,
-                h, ga, dpre, gy, dqkv, ctx, gt, rt, vec, part, y, gx, buf, isem, osem):
+                h, ga, dpre, gy, dqkv, ctx, gt, rt, vec, part, y, gx, buf, small, isem, osem, ssem):
     n_heads, head = dbqkv_o.shape[1], dbqkv_o.shape[2]
-    block = 320
-    slots = buf.shape[0]
-    pairs = ((rt_h, rt), (gy_h, gy), (gt_h, gt), (dpre_h, dpre), (dqkv_h, dqkv), (h_h, h), (ctx_h, ctx), (ga_h, ga), (vec_h, vec),
+    slots, block = buf.shape[0], buf.shape[1]
+    pairs = ((ctx_h, ctx), (ga_h, ga), (rt_h, rt), (gy_h, gy), (gt_h, gt), (dpre_h, dpre), (dqkv_h, dqkv), (h_h, h), (vec_h, vec),
              (part_h, part), (y_h, y), (gx_h, gx))
     loads = []
 
@@ -484,24 +484,43 @@
             loads.append(copy)
 
     fetch(2)
-    step = 0
-    pending = []
-    for n, (left, right, out) in enumerate(((rt, gy, dwdn_o), (gt, dpre, dwup_o), (dqkv, h, dwqkv_o), (ctx, ga, dwout_o))):
-        loads[2 * n].wait()
-        loads[2 * n + 1].wait()
-        if n == 0:
-            fetch(len(pairs))
-        rv = right[...]
-        for m in range(left.shape[0] // block):
-            s = step % slots
-            if step >= slots:
-                pending[step - slots].wait()
-            mm = slice(m * block, (m + 1) * block)
-            buf[s] = dot(left[mm, :], rv).astype(BF)
-            copy = pltpu.make_async_copy(buf.at[s], out.at[pl.ds(m * block, block), :], osem.at[s])
-            copy.start()
-            pending.append(copy)
-            step += 1
+    for copy in loads:
+        copy.wait()
+    fetch(len(pairs))
+    tail = []
+
+    def piece(k, start, size):
+        small[k, pl.ds(0, size), :] = dot(ctx[start:start + size, :], ga[...]).astype(BF)
+        copy = pltpu.make_async_copy(small.at[k, pl.ds(0, size), :], dwout_o.at[pl.ds(start, size), :], ssem.at[k])
+        copy.start()
+        tail.append(copy)
+
+    def written(slot, out):
+        return pltpu.make_async_copy(buf.at[slot], out.at[pl.ds(0, block), :], osem.at[slot])
+
+    piece(0, 0, 160)
+    first = 0
+    for n, (left, right, out) in enumerate(((rt, gy, dwdn_o), (gt, dpre, dwup_o), (dqkv, h, dwqkv_o))):
+        loads[2 * n + 2].wait()
+        loads[2 * n + 3].wait()
+
+        def body(m, carry, left=left, right=right, out=out, first=first):
+            slot = lax.rem(first + m, slots)
+
+            @pl.when(first + m >= slots)
+            def _():
+                written(slot, out).wait()
+
+            at = pl.ds(pl.multiple_of(m * block, block), block)
+            buf[slot] = dot(left[at, :], right[...]).astype(BF)
+            pltpu.make_async_copy(buf.at[slot], out.at[at, :], osem.at[slot]).start()
+            return carry
+
+        count = left.shape[0] // block
+        lax.fori_loop(0, count, body, 0)
+        first += count
+    piece(1, 160, 320)
+    piece(2, 480, 160)
     ones = jnp.ones((8, dqkv.shape[1]), BF)
     sums = dot_t(ones, dqkv[...])[0:1]
     for k in range(3):
@@ -516,8 +535,10 @@
         o[...] = (part[0, k, :] + part[1, k, :]) + (part[2, k, :] + part[3, k, :])
     for k, o in enumerate((v2, v3, v4, v5, v6)):
         o[...] = vec[2 + k, :]
-    for k in range(max(0, step - slots), step):
-        pending[k].wait()
+    for k in range(slots):
+        written(k, dwqkv_o).wait()
+    for copy in tail:
+        copy.wait()
 
 
 def solution(mesh):
@@ -571,8 +592,8 @@
             out_specs=[any_spec] * 4 + [vspec] * 10,
             scratch_shapes=[
                 vm((S, D), BF), vm((S, D), BF), vm((S, FL), BF), vm((S, D), BF), vm((Q, S), BF), vm((C, S), BF), vm((D, S), BF),
-                vm((FL, S), BF), vm((8, D), F32), vm((TP, 2, D), F32), vm((S // TP, D), BF), vm((S // TP, D), BF), vm((4, 320, D), BF),
-                pltpu.SemaphoreType.DMA((12,)), pltpu.SemaphoreType.DMA((4,)),
+                vm((FL, S), BF), vm((8, D), F32), vm((TP, 2, D), F32), vm((S // TP, D), BF), vm((S // TP, D), BF), vm((3, 640, D), BF), vm((3, 320, D), BF),
+                pltpu.SemaphoreType.DMA((12,)), pltpu.SemaphoreType.DMA((3,)), pltpu.SemaphoreType.DMA((3,)),
             ],
             compiler_params=pltpu.CompilerParams(vmem_limit_bytes=60 * 1024 * 1024),
         )(h, ga, dpre, gyf, dqkv, ctx, gt, rt, vec, part, y, gx)

time: 71.4 us -> 71 us (level)
  no operation moved by 1% of the time
where the time goes in v4:
time: 71 us; the launch traced here: 70.9 us
  Pallas kernels  70.1 us (99%)
  between operations  0.82 us (1%)
    pallas_call x1, Pallas kernels, local_step(): pl.pallas_call(layer_kernel, name='layer', out_shape=[sds((S // TP, D), B...  53.2 us
    pallas_call x1, Pallas kernels, local_step(): pl.pallas_call(grad_kernel, name='weight_grads', out_shape=[sds((Q, D), B...  16.9 us

profile of v4, /device:TPU:0, one launch (start us, length us, event | category | flops | bytes accessed | tf_op | source)
XLA Modules:
  0.0 70.9 jit_solution(13428039819410860368)
XLA Ops:
  0.7 53.2 %layer.1 = (bf16[32,2560]{1,0:T(8,128)(2,1)}, bf16[32,2560]{1,0:T(8,128)(2,1)}, f32[8,2560]{1,0:T(8,128)}, f32[4,2,2560]{2,1,0:T(2,128)}, bf16[128,2560]{1,0:T(8...) custom-call(bf16[32,2560]{1,0:T(8,128)(2,1)} %bitcast.13, ...), custom_call_target="tpu_custom_call" | custom-call | tf_op jit(solution)/shard_map/layer/pallas_call | solution.py:562
  53.8 16.9 %weight_grads.1 = (bf16[1920,2560]{1,0:T(8,128)(2,1)}, bf16[640,2560]{1,0:T(8,128)(2,1)}, bf16[2560,2560]{1,0:T(8,128)(2,1)}, bf16[2560,2560]{1,0:T(8,128)(2,1)}...) custom-call(bf16[128,2560]{1,0:T(8,128)(2,1)} %get-tuple-element.40., ...), custom_call_target="tpu_custom_call" | custom-call | tf_op jit(solution)/shard_map/weight_grads/pallas_call | solution.py:586

commit v5 on v4

--- a/solution.py
+++ b/solution.py
@@ -19,8 +19,9 @@
 ALL_CHUNKS = (2, 4, 4, 5, 4, 1)
 SCATTER_CHUNKS = (6, 6, 5, 3)
 N_BLK = 5
+LAYER_VMEM = 59 * 1024 * 1024
+GRAD_VMEM = 24 * 1024 * 1024
 N_REMOTE = 59
-N_STORE = 12
 
 
 def alibi_slopes(n_heads):
@@ -41,11 +42,11 @@
 
 
 def layer_kernel(x_h, gy_h, wqkv_h, bqkv_h, wout_h, wup_h, wdn_h, ln1g_h, ln1b_h, ln2g_h, ln2b_h, bout_h, bdown_h, bup_h,
-                 y_o, gx_o, vec_o, part_o, h_o, ga_o, dpre_o, gy_o, dqkv_o, ctx_o, gt_o, rt_o,
-                 wqkv, wout, wup, wdn, bqkv, vecs, xg, gyg, h, bias, qkv, prob, probb, ctx, x1, xhat, g, gt, rt, gact, r, dpre,
-                 gmid, ga, dctx, dqkv, ybuf, gxbuf, xh1, vec, part, ubuf, xr, vt, dpb, dsb,
+                 ybuf, gxbuf, vec, part_o, h, ga, dpre, gy_o, dqkv, ctx, gt, rt,
+                 wqkv, wout, wup, wdn, bqkv, vecs, xg, gyg, bias, qkv, prob, probb, x1, xhat, g, gact, r,
+                 gmid, dctx, xh1, ubuf, xr, vt, dpb, dsb,
                  p1, rd1, s1, rs1, t1, q1, e1, p2, rd2, s2, rs2, t2, q2, e2, py, rdy, sy, rsy, ph, rdh, sh, rsh,
-                 lsem, osem, ssem, rsem):
+                 lsem, ssem, rsem):
     D = x_h.shape[1]
     seq = TP * 32
     head = bqkv_h.shape[2]
@@ -70,7 +71,7 @@
     blk_own = pl.ds(pl.multiple_of(chip * 32, 32), 32)
     blk_cross = pl.ds(pl.multiple_of((1 - chip) * 32, 32), 32)
 
-    counter = [0, 0, 0]
+    counter = [0, 0]
 
     def load(src, dst):
         k = counter[0]
@@ -79,20 +80,11 @@
         copy.start()
         return copy
 
-    outs = []
-
-    def store(src, dst):
+    sent = []
+
+    def remote(src, dst, dev):
         k = counter[1]
         counter[1] += 1
-        copy = pltpu.make_async_copy(src, dst, osem.at[k])
-        copy.start()
-        outs.append(copy)
-
-    sent = []
-
-    def remote(src, dst, dev):
-        k = counter[2]
-        counter[2] += 1
         copy = pltpu.make_async_remote_copy(src_ref=src, dst_ref=dst, send_sem=ssem.at[k], recv_sem=rsem.at[k],
                                             device_id={'tp': dev}, device_id_type=MESH)
         copy.start()
@@ -275,8 +267,6 @@
         sum_a.put(j)
     for j in range(n_all):
         sum_a.step_cross(j)
-    store(h, h_o)
-    store(ctx, ctx_o)
 
     gy_to_sib.wait_recv()
     gy_to_cross.wait_recv()
@@ -284,7 +274,7 @@
     for hd in range(n_heads):
         vt[hd] = qkv[part_of(hd, 2), :].T
     gy_fwd.wait_recv()
-    store(gyg, gy_o)
+    gy_o[...] = gyg[...]
     lwdn.wait()
     lwup.wait()
     fw = wdn_h.shape[0] // N_BLK
@@ -333,7 +323,7 @@
         r[:, ff] = (hp + hp * th).astype(BF)
         slope_g = (0.5 + 0.5 * th) + (hp * (1.0 - th * th)) * (GELU_C + 3.0 * w)
         gp = gact[:, ff].astype(F32) * slope_g
-        vec[6:7, ff] = jnp.sum(gp, axis=0, keepdims=True)
+        vec[6, :, ff] = jnp.sum(gp, axis=0, keepdims=True)
         dpre[:, ff] = gp.astype(BF)
 
     dv = dpre[...]
@@ -344,7 +334,6 @@
         if j:
             sum_g.step_cross(j - 1)
     sum_g.step_cross(n_all - 1)
-    store(dpre, dpre_o)
 
     acc1 = jnp.zeros((seq, LANES), F32)
     acc2 = jnp.zeros((seq, LANES), F32)
@@ -355,8 +344,8 @@
             dg = t2[:, lc(c)].astype(F32)
             z = xhat[:, lc(c)]
             dgz = dg * z
-            vec[2:3, lc(c)] = jnp.sum(dgz, axis=0, keepdims=True)
-            vec[3:4, lc(c)] = jnp.sum(dg, axis=0, keepdims=True)
+            vec[2, :, lc(c)] = jnp.sum(dgz, axis=0, keepdims=True)
+            vec[3, :, lc(c)] = jnp.sum(dg, axis=0, keepdims=True)
             gain = vecs[2, :, lc(c)]
             dz = dg * gain
             acc1 = acc1 + dz
@@ -374,13 +363,11 @@
             for c in range(j * (yw // LANES), (j + 1) * (yw // LANES)):
                 gt[lc(c), :] = g[:, lc(c)].T
                 rt[lc(c), :] = r[:, lc(c)].T
-                vec[5:6, lc(c)] = jnp.sum(gyg[:, lc(c)].astype(F32), axis=0, keepdims=True)
+                vec[5, :, lc(c)] = jnp.sum(gyg[:, lc(c)].astype(F32), axis=0, keepdims=True)
                 for n, hh in enumerate(halves):
                     xr[hh, lc(c)] = xhat[hh, lc(c)] * rstd2[n]
         if j == N_BLK:
             y_sib = remote(py.at[sibhalf, :], rdy, sib)
-            store(gt, gt_o)
-            store(rt, rt_o)
         sum_g.step_back(j)
         if j:
             acc1, acc2 = ln2_back_chunk(j - 1, acc1, acc2)
@@ -426,17 +413,13 @@
         if j:
             sum_h.step_cross(j - 1)
     sum_h.step_cross(n_scat - 1)
-    store(ga, ga_o)
-    store(dqkv, dqkv_o)
 
     rstd1 = ln_block(own, 32, xg, 0, 1, None)
     y_cross.wait_recv()
     for c in range(nlc):
         z = (sy[blk_own, lc(c)].astype(F32) + rsy[:, lc(c)].astype(F32)).astype(BF).astype(F32)
         ybuf[:, lc(c)] = (x1[own, lc(c)] + z + vecs[5, :, lc(c)]).astype(BF)
-        vec[4:5, lc(c)] = jnp.sum(gmid[:, lc(c)], axis=0, keepdims=True)
-    store(ybuf, y_o)
-    store(vec, vec_o)
+        vec[4, :, lc(c)] = jnp.sum(gmid[:, lc(c)], axis=0, keepdims=True)
 
     me = slot(t)
     acc1 = jnp.zeros((32, LANES), F32)
@@ -447,46 +430,28 @@
             dh = sum_h.result(lc(c))
             z = xh1[:, lc(c)]
             dhz = dh * z
-            part[0:1, lc(c)] = jnp.sum(dhz, axis=0, keepdims=True)
-            part[1:2, lc(c)] = jnp.sum(dh, axis=0, keepdims=True)
+            part_o[me, 0:1, lc(c)] = jnp.sum(dhz, axis=0, keepdims=True)
+            part_o[me, 1:2, lc(c)] = jnp.sum(dh, axis=0, keepdims=True)
             gain = vecs[0, :, lc(c)]
             acc1 = acc1 + dh * gain
             acc2 = acc2 + dhz * gain
-    parts = [remote(part, part_o.at[me], dev) for dev in (cross, sibcross, sib)]
-    store(part, part_o.at[me])
+    parts = [remote(part_o.at[me], part_o.at[me], dev) for dev in (cross, sibcross, sib)]
     mean1 = jnp.sum(acc1, axis=1, keepdims=True) / D
     mean2 = jnp.sum(acc2, axis=1, keepdims=True) / D
     for c in range(nlc):
         dz = sum_h.result(lc(c)) * vecs[0, :, lc(c)]
         gxbuf[:, lc(c)] = (gmid[own, lc(c)] + rstd1 * (dz - mean1 - xh1[:, lc(c)] * mean2)).astype(BF)
-    store(gxbuf, gx_o)
     for copy in sent:
         copy.wait_send()
-    for copy in outs:
-        copy.wait()
     for copy in parts:
         copy.wait_recv()
 
 
-def grad_kernel(h_h, ga_h, dpre_h, gy_h, dqkv_h, ctx_h, gt_h, rt_h, vec_h, part_h, y_h, gx_h,
+def grad_kernel(h, ga, dpre, gy, dqkv, ctx, gt, rt, vec, part, y, gx,
                 dwqkv_o, dwout_o, dwup_o, dwdn_o, dbqkv_o, y_o, gx_o, v0, v1, v2, v3, v4, v5, v6,
-                h, ga, dpre, gy, dqkv, ctx, gt, rt, vec, part, y, gx, buf, small, isem, osem, ssem):
+                buf, small, sums, bq, osem, ssem):
     n_heads, head = dbqkv_o.shape[1], dbqkv_o.shape[2]
     slots, block = buf.shape[0], buf.shape[1]
-    pairs = ((ctx_h, ctx), (ga_h, ga), (rt_h, rt), (gy_h, gy), (gt_h, gt), (dpre_h, dpre), (dqkv_h, dqkv), (h_h, h), (vec_h, vec),
-             (part_h, part), (y_h, y), (gx_h, gx))
-    loads = []
-
-    def fetch(n):
-        for src, dst in pairs[len(loads):n]:
-            copy = pltpu.make_async_copy(src, dst, isem.at[len(loads)])
-            copy.start()
-            loads.append(copy)
-
-    fetch(2)
-    for copy in loads:
-        copy.wait()
-    fetch(len(pairs))
     tail = []
 
     def piece(k, start, size):
@@ -499,10 +464,22 @@
         return pltpu.make_async_copy(buf.at[slot], out.at[pl.ds(0, block), :], osem.at[slot])
 
     piece(0, 0, 160)
+    for k in range(2):
+        sums[k] = (part[0, k:k + 1, :] + part[1, k:k + 1, :]) + (part[2, k:k + 1, :] + part[3, k:k + 1, :])
+
+    def send(src, dst):
+        copy = pltpu.make_async_copy(src, dst, ssem.at[len(tail) + 2])
+        copy.start()
+        tail.append(copy)
+
+    send(y, y_o)
+    send(gx, gx_o)
+    for k, o in enumerate((v2, v3, v4, v5, v6)):
+        send(vec.at[k + 2, 0], o)
+    for k, o in enumerate((v0, v1)):
+        send(sums.at[k, 0], o)
     first = 0
-    for n, (left, right, out) in enumerate(((rt, gy, dwdn_o), (gt, dpre, dwup_o), (dqkv, h, dwqkv_o))):
-        loads[2 * n + 2].wait()
-        loads[2 * n + 3].wait()
+    for left, right, out in ((rt, gy, dwdn_o), (gt, dpre, dwup_o), (dqkv, h, dwqkv_o)):
 
         def body(m, carry, left=left, right=right, out=out, first=first):
             slot = lax.rem(first + m, slots)
@@ -520,21 +497,14 @@
         lax.fori_loop(0, count, body, 0)
         first += count
     piece(1, 160, 320)
-    piece(2, 480, 160)
     ones = jnp.ones((8, dqkv.shape[1]), BF)
-    sums = dot_t(ones, dqkv[...])[0:1]
+    total = dot_t(ones, dqkv[...])[0:1]
     for k in range(3):
         for hd in range(n_heads):
             at = (hd * 3 + k) * head
-            dbqkv_o[k, hd:hd + 1, :] = sums[:, at:at + head]
-    for k in range(8, 12):
-        loads[k].wait()
-    y_o[...] = y[...]
-    gx_o[...] = gx[...]
-    for k, o in enumerate((v0, v1)):
-        o[...] = (part[0, k, :] + part[1, k, :]) + (part[2, k, :] + part[3, k, :])
-    for k, o in enumerate((v2, v3, v4, v5, v6)):
-        o[...] = vec[2 + k, :]
+            bq[k, hd:hd + 1, :] = total[:, at:at + head]
+    send(bq, dbqkv_o)
+    piece(2, 480, 160)
     for k in range(slots):
         written(k, dwqkv_o).wait()
     for copy in tail:
@@ -550,6 +520,7 @@
         C = nh * head
         FL = w_up.shape[1]
         any_spec = pl.BlockSpec(memory_space=pl.ANY)
+        vspec = pl.BlockSpec(memory_space=pltpu.VMEM)
         vm = pltpu.VMEM
         wqkv_t = jnp.transpose(w_qkv, (1, 2, 3, 0)).reshape(Q, D)
         bq = jnp.transpose(b_qkv, (1, 0, 2))
@@ -562,40 +533,38 @@
         res = pl.pallas_call(
             layer_kernel,
             name='layer',
-            out_shape=[sds((S // TP, D), BF), sds((S // TP, D), BF), sds((8, D), F32), sds((TP, 2, D), F32), sds((S, D), BF), sds((S, D), BF),
-                       sds((S, FL), BF), sds((S, D), BF), sds((Q, S), BF), sds((C, S), BF), sds((D, S), BF), sds((FL, S), BF)],
+            out_shape=[vm((S // TP, D), BF), vm((S // TP, D), BF), vm((7, 1, D), F32), vm((TP, 2, D), F32), vm((S, D), BF), vm((S, D), BF),
+                       vm((S, FL), BF), vm((S, D), BF), vm((Q, S), BF), vm((C, S), BF), vm((D, S), BF), vm((FL, S), BF)],
             in_specs=[any_spec] * 14,
-            out_specs=[any_spec] * 12,
+            out_specs=[vspec] * 12,
             scratch_shapes=[
                 vm((Q, D), BF), vm((C, D), BF), vm((D, FL), BF), vm((FL, D), BF), vm((3, nh, head), F32), vm((7, 1, D), F32),
-                vm((S, D), BF), vm((S, D), BF), vm((S, D), BF), vm((Q, S), F32), vm((Q, S), BF), vm((nh, S, S), F32),
-                vm((nh, S, S), BF), vm((C, S), BF), vm((S, D), F32), vm((S, D), F32), vm((S, D), BF), vm((D, S), BF), vm((FL, S), BF),
-                vm((S, FL), BF), vm((S, FL), BF), vm((S, FL), BF), vm((S, D), F32), vm((S, D), BF), vm((C, S), BF), vm((Q, S), BF),
-                vm((S // TP, D), BF), vm((S // TP, D), BF), vm((S // TP, D), F32), vm((8, D), F32), vm((2, D), F32), vm((S, D), F32), vm((S, D), F32),
+                vm((S, D), BF), vm((S, D), BF), vm((Q, S), F32), vm((Q, S), BF), vm((nh, S, S), F32),
+                vm((nh, S, S), BF), vm((S, D), F32), vm((S, D), F32), vm((S, D), BF),
+                vm((S, FL), BF), vm((S, FL), BF), vm((S, D), F32), vm((C, S), BF),
+                vm((S // TP, D), F32), vm((S, D), F32), vm((S, D), F32),
                 vm((nh, S, head), BF), vm((nh, S, S), BF), vm((nh, S, S), BF),
                 *red, *red, *scat, *scat,
-                pltpu.SemaphoreType.DMA((n_loads,)), pltpu.SemaphoreType.DMA((N_STORE,)),
+                pltpu.SemaphoreType.DMA((n_loads,)),
                 pltpu.SemaphoreType.DMA((N_REMOTE,)), pltpu.SemaphoreType.DMA((N_REMOTE,)),
             ],
-            compiler_params=pltpu.CompilerParams(collective_id=0, has_side_effects=True, vmem_limit_bytes=67043328),
+            compiler_params=pltpu.CompilerParams(collective_id=0, has_side_effects=True, vmem_limit_bytes=LAYER_VMEM),
         )(x.reshape(x.shape[1], D), grad_y.reshape(x.shape[1], D), wqkv_t, bq, w_out, w_up, w_down, row(ln1_gamma), row(ln1_beta),
           row(ln2_gamma), row(ln2_beta), row(b_out), row(b_down), row(b_up))
         y, gx, vec, part, h, ga, dpre, gyf, dqkv, ctx, gt, rt = res
-        vspec = pl.BlockSpec(memory_space=pltpu.VMEM)
         vshape = sds((D,), F32)
         outs = pl.pallas_call(
             grad_kernel,
             name='weight_grads',
             out_shape=[sds((Q, D), BF), sds((C, D), BF), sds((D, FL), BF), sds((FL, D), BF), sds((3, nh, head), F32),
                        sds((S // TP, D), BF), sds((S // TP, D), BF)] + [vshape] * 7,
-            in_specs=[any_spec] * 12,
-            out_specs=[any_spec] * 4 + [vspec] * 10,
+            in_specs=[vspec] * 12,
+            out_specs=[any_spec] * 14,
             scratch_shapes=[
-                vm((S, D), BF), vm((S, D), BF), vm((S, FL), BF), vm((S, D), BF), vm((Q, S), BF), vm((C, S), BF), vm((D, S), BF),
-                vm((FL, S), BF), vm((8, D), F32), vm((TP, 2, D), F32), vm((S // TP, D), BF), vm((S // TP, D), BF), vm((3, 640, D), BF), vm((3, 320, D), BF),
-                pltpu.SemaphoreType.DMA((12,)), pltpu.SemaphoreType.DMA((3,)), pltpu.SemaphoreType.DMA((3,)),
+                vm((3, 640, D), BF), vm((3, 320, D), BF), vm((2, 1, D), F32), vm((3, nh, head), F32),
+                pltpu.SemaphoreType.DMA((3,)), pltpu.SemaphoreType.DMA((14,)),
             ],
-            compiler_params=pltpu.CompilerParams(vmem_limit_bytes=60 * 1024 * 1024),
+            compiler_params=pltpu.CompilerParams(vmem_limit_bytes=GRAD_VMEM),
         )(h, ga, dpre, gyf, dqkv, ctx, gt, rt, vec, part, y, gx)
         dwqkv, dwout, dwup, dwdn, dbqkv, y, gx, g_ln1g, g_ln1b, g_ln2g, g_ln2b, g_bout, g_bdown, g_bup = outs
         dwqkv = jnp.transpose(dwqkv.reshape(nh, 3, head, D), (3, 0, 1, 2))

time: 71 us -> 67.8 us (0.955)
  Pallas kernels: 70.1 us -> 66.9 us
    pallas_call x1, Pallas kernels: 16.9 us -> 13.9 us  [local_step(): pl.pallas_call(grad_kernel, name='weight_grads', out_shape=[sds((Q, D), B...]
where the time goes in v5:
time: 67.8 us; the launch traced here: 67.7 us
  Pallas kernels  66.9 us (99%)
  between operations  0.82 us (1%)
    pallas_call x1, Pallas kernels, local_step(): pl.pallas_call(layer_kernel, name='layer', out_shape=[vm((S // TP, D), BF...  53 us
    pallas_call x1, Pallas kernels, local_step(): pl.pallas_call(grad_kernel, name='weight_grads', out_shape=[sds((Q, D), B...  13.9 us

profile of v5, /device:TPU:0, one launch (start us, length us, event | category | flops | bytes accessed | tf_op | source)
XLA Modules:
  0.0 67.7 jit_solution(15314803176995173272)
XLA Ops:
  0.7 53.0 %layer.1 = (bf16[32,2560]{1,0:T(8,128)(2,1)S(1)}, bf16[32,2560]{1,0:T(8,128)(2,1)S(1)}, f32[7,1,2560]{2,1,0:T(1,128)S(1)}, f32[4,2,2560]{2,1,0:T(2,128)S(1)}, bf...) custom-call(bf16[32,2560]{1,0:T(8,128)(2,1)} %bitcast.13, ...), custom_call_target="tpu_custom_call" | custom-call | tf_op jit(solution)/shard_map/layer/pallas_call | solution.py:533
  53.6 13.9 %weight_grads.1 = (bf16[1920,2560]{1,0:T(8,128)(2,1)}, bf16[640,2560]{1,0:T(8,128)(2,1)}, bf16[2560,2560]{1,0:T(8,128)(2,1)}, bf16[2560,2560]{1,0:T(8,128)(2,1)}...) custom-call(bf16[128,2560]{1,0:T(8,128)(2,1)S(1)} %get-tuple-element, ...), custom_call_target="tpu_custom_call" | custom-call | tf_op jit(solution)/shard_map/weight_grads/pallas_call | solution.py:556

commit v6 on v5

--- a/solution.py
+++ b/solution.py
@@ -17,11 +17,13 @@
 TP = 4
 LANES = 128
 ALL_CHUNKS = (2, 4, 4, 5, 4, 1)
-SCATTER_CHUNKS = (6, 6, 5, 3)
+SCATTER_CHUNKS = (2, 6, 8, 4)
 N_BLK = 5
-LAYER_VMEM = 59 * 1024 * 1024
+GRAD_ROWS = 640
+WORK_CUTS = (0, 3, 5, 6, 7, 7, 7)
+LAYER_VMEM = 47 * 1024 * 1024
 GRAD_VMEM = 24 * 1024 * 1024
-N_REMOTE = 59
+N_REMOTE = 62
 
 
 def alibi_slopes(n_heads):
@@ -42,8 +44,8 @@
 
 
 def layer_kernel(x_h, gy_h, wqkv_h, bqkv_h, wout_h, wup_h, wdn_h, ln1g_h, ln1b_h, ln2g_h, ln2b_h, bout_h, bdown_h, bup_h,
-                 ybuf, gxbuf, vec, part_o, h, ga, dpre, gy_o, dqkv, ctx, gt, rt,
-                 wqkv, wout, wup, wdn, bqkv, vecs, xg, gyg, bias, qkv, prob, probb, x1, xhat, g, gact, r,
+                 ybuf, gxbuf, vec, part_o, h, ga, dpre, dqkv, ctx, gt, wdn,
+                 wqkv, wout, wup, rt, bqkv, vecs, xg, gyg, bias, qkv, prob, probb, x1, xhat, g, gact, r,
                  gmid, dctx, xh1, ubuf, xr, vt, dpb, dsb,
                  p1, rd1, s1, rs1, t1, q1, e1, p2, rd2, s2, rs2, t2, q2, e2, py, rdy, sy, rsy, ph, rdh, sh, rsh,
                  lsem, ssem, rsem):
@@ -274,7 +276,6 @@
     for hd in range(n_heads):
         vt[hd] = qkv[part_of(hd, 2), :].T
     gy_fwd.wait_recv()
-    gy_o[...] = gyg[...]
     lwdn.wait()
     lwup.wait()
     fw = wdn_h.shape[0] // N_BLK
@@ -329,7 +330,8 @@
     dv = dpre[...]
     sum_g = AllSum(p2, rd2, s2, rs2, t2, q2, e2)
     for j in range(n_all):
-        sum_g.fill(j, dot_t(dv, wup[sum_g.ch(j), :]).astype(BF))
+        for c in [lc(c) for c in groups(ALL_CHUNKS, j)] if j == 0 else [sum_g.ch(j)]:
+            p2[:, c] = dot_t(dv, wup[c, :]).astype(BF)
         sum_g.put(j)
         if j:
             sum_g.step_cross(j - 1)
@@ -354,19 +356,27 @@
                 ubuf[hh, lc(c)] = gyg[hh, lc(c)].astype(F32) + rstd2[n] * dz[hh]
         return acc1, acc2
 
-    rv = r[...]
     yw = D // N_BLK
+
+    def down(j):
+        yy = slice(j * yw, (j + 1) * yw)
+        py[:, yy] = dot(r[...], wdn[:, yy]).astype(BF)
+        for c in range(j * (yw // LANES), (j + 1) * (yw // LANES)):
+            gt[lc(c), :] = g[:, lc(c)].T
+            rt[lc(c), :] = r[:, lc(c)].T
+            vec[5, :, lc(c)] = jnp.sum(gyg[:, lc(c)].astype(F32), axis=0, keepdims=True)
+            for n, hh in enumerate(halves):
+                xr[hh, lc(c)] = xhat[hh, lc(c)] * rstd2[n]
+
+    def grad_down(m):
+        mm = slice(m * GRAD_ROWS, (m + 1) * GRAD_ROWS)
+        wdn[mm, :] = dot(rt[mm, :], gyg[...]).astype(BF)
+
+    work = [(down, k) for k in range(N_BLK)] + [(grad_down, m) for m in range(wdn.shape[0] // GRAD_ROWS)]
     for j in range(n_all):
-        if j < N_BLK:
-            yy = slice(j * yw, (j + 1) * yw)
-            py[:, yy] = dot(rv, wdn[:, yy]).astype(BF)
-            for c in range(j * (yw // LANES), (j + 1) * (yw // LANES)):
-                gt[lc(c), :] = g[:, lc(c)].T
-                rt[lc(c), :] = r[:, lc(c)].T
-                vec[5, :, lc(c)] = jnp.sum(gyg[:, lc(c)].astype(F32), axis=0, keepdims=True)
-                for n, hh in enumerate(halves):
-                    xr[hh, lc(c)] = xhat[hh, lc(c)] * rstd2[n]
-        if j == N_BLK:
+        for step, m in work[WORK_CUTS[j]:WORK_CUTS[j + 1]]:
+            step(m)
+        if j == 1:
             y_sib = remote(py.at[sibhalf, :], rdy, sib)
         sum_g.step_back(j)
         if j:
@@ -408,7 +418,8 @@
     n_scat = len(SCATTER_CHUNKS)
     dq = dqkv[...].T
     for j in range(n_scat):
-        sum_h.fill(j, dot(dq, wqkv[:, sum_h.ch(j)]).astype(BF))
+        for c in [lc(c) for c in groups(SCATTER_CHUNKS, j)] if j == 0 else [sum_h.ch(j)]:
+            ph[:, c] = dot(dq, wqkv[:, c]).astype(BF)
         sum_h.put(j)
         if j:
             sum_h.step_cross(j - 1)
@@ -424,6 +435,9 @@
     me = slot(t)
     acc1 = jnp.zeros((32, LANES), F32)
     acc2 = jnp.zeros((32, LANES), F32)
+    parts = []
+    for step, m in work[WORK_CUTS[-1]:]:
+        step(m)
     for j in range(n_scat):
         sum_h.b[j].wait_recv()
         for c in groups(SCATTER_CHUNKS, j):
@@ -435,7 +449,9 @@
             gain = vecs[0, :, lc(c)]
             acc1 = acc1 + dh * gain
             acc2 = acc2 + dhz * gain
-    parts = [remote(part_o.at[me], part_o.at[me], dev) for dev in (cross, sibcross, sib)]
+        if j >= n_scat - 2:
+            c = slice(0, sum_h.ch(j).stop) if j == n_scat - 2 else sum_h.ch(j)
+            parts += [remote(part_o.at[me, :, c], part_o.at[me, :, c], dev) for dev in (cross, sibcross, sib)]
     mean1 = jnp.sum(acc1, axis=1, keepdims=True) / D
     mean2 = jnp.sum(acc2, axis=1, keepdims=True) / D
     for c in range(nlc):
@@ -447,7 +463,7 @@
         copy.wait_recv()
 
 
-def grad_kernel(h, ga, dpre, gy, dqkv, ctx, gt, rt, vec, part, y, gx,
+def grad_kernel(h, ga, dpre, dqkv, ctx, gt, dwdn, vec, part, y, gx,
                 dwqkv_o, dwout_o, dwup_o, dwdn_o, dbqkv_o, y_o, gx_o, v0, v1, v2, v3, v4, v5, v6,
                 buf, small, sums, bq, osem, ssem):
     n_heads, head = dbqkv_o.shape[1], dbqkv_o.shape[2]
@@ -463,12 +479,17 @@
     def written(slot, out):
         return pltpu.make_async_copy(buf.at[slot], out.at[pl.ds(0, block), :], osem.at[slot])
 
+    for k in range(4):
+        n = dwdn.shape[0] // 4
+        copy = pltpu.make_async_copy(dwdn.at[pl.ds(k * n, n), :], dwdn_o.at[pl.ds(k * n, n), :], ssem.at[14 + k])
+        copy.start()
+        tail.append(copy)
     piece(0, 0, 160)
     for k in range(2):
         sums[k] = (part[0, k:k + 1, :] + part[1, k:k + 1, :]) + (part[2, k:k + 1, :] + part[3, k:k + 1, :])
 
     def send(src, dst):
-        copy = pltpu.make_async_copy(src, dst, ssem.at[len(tail) + 2])
+        copy = pltpu.make_async_copy(src, dst, ssem.at[len(tail) - 2])
         copy.start()
         tail.append(copy)
 
@@ -479,7 +500,7 @@
     for k, o in enumerate((v0, v1)):
         send(sums.at[k, 0], o)
     first = 0
-    for left, right, out in ((rt, gy, dwdn_o), (gt, dpre, dwup_o), (dqkv, h, dwqkv_o)):
+    for left, right, out in ((gt, dpre, dwup_o), (dqkv, h, dwqkv_o)):
 
         def body(m, carry, left=left, right=right, out=out, first=first):
             slot = lax.rem(first + m, slots)
@@ -534,11 +555,11 @@
             layer_kernel,
             name='layer',
             out_shape=[vm((S // TP, D), BF), vm((S // TP, D), BF), vm((7, 1, D), F32), vm((TP, 2, D), F32), vm((S, D), BF), vm((S, D), BF),
-                       vm((S, FL), BF), vm((S, D), BF), vm((Q, S), BF), vm((C, S), BF), vm((D, S), BF), vm((FL, S), BF)],
+                       vm((S, FL), BF), vm((Q, S), BF), vm((C, S), BF), vm((D, S), BF), vm((FL, D), BF)],
             in_specs=[any_spec] * 14,
-            out_specs=[vspec] * 12,
+            out_specs=[vspec] * 11,
             scratch_shapes=[
-                vm((Q, D), BF), vm((C, D), BF), vm((D, FL), BF), vm((FL, D), BF), vm((3, nh, head), F32), vm((7, 1, D), F32),
+                vm((Q, D), BF), vm((C, D), BF), vm((D, FL), BF), vm((FL, S), BF), vm((3, nh, head), F32), vm((7, 1, D), F32),
                 vm((S, D), BF), vm((S, D), BF), vm((Q, S), F32), vm((Q, S), BF), vm((nh, S, S), F32),
                 vm((nh, S, S), BF), vm((S, D), F32), vm((S, D), F32), vm((S, D), BF),
                 vm((S, FL), BF), vm((S, FL), BF), vm((S, D), F32), vm((C, S), BF),
@@ -551,21 +572,21 @@
             compiler_params=pltpu.CompilerParams(collective_id=0, has_side_effects=True, vmem_limit_bytes=LAYER_VMEM),
         )(x.reshape(x.shape[1], D), grad_y.reshape(x.shape[1], D), wqkv_t, bq, w_out, w_up, w_down, row(ln1_gamma), row(ln1_beta),
           row(ln2_gamma), row(ln2_beta), row(b_out), row(b_down), row(b_up))
-        y, gx, vec, part, h, ga, dpre, gyf, dqkv, ctx, gt, rt = res
+        y, gx, vec, part, h, ga, dpre, dqkv, ctx, gt, dwdn = res
         vshape = sds((D,), F32)
         outs = pl.pallas_call(
             grad_kernel,
             name='weight_grads',
             out_shape=[sds((Q, D), BF), sds((C, D), BF), sds((D, FL), BF), sds((FL, D), BF), sds((3, nh, head), F32),
                        sds((S // TP, D), BF), sds((S // TP, D), BF)] + [vshape] * 7,
-            in_specs=[vspec] * 12,
+            in_specs=[vspec] * 11,
             out_specs=[any_spec] * 14,
             scratch_shapes=[
                 vm((3, 640, D), BF), vm((3, 320, D), BF), vm((2, 1, D), F32), vm((3, nh, head), F32),
-                pltpu.SemaphoreType.DMA((3,)), pltpu.SemaphoreType.DMA((14,)),
+                pltpu.SemaphoreType.DMA((3,)), pltpu.SemaphoreType.DMA((18,)),
             ],
             compiler_params=pltpu.CompilerParams(vmem_limit_bytes=GRAD_VMEM),
-        )(h, ga, dpre, gyf, dqkv, ctx, gt, rt, vec, part, y, gx)
+        )(h, ga, dpre, dqkv, ctx, gt, dwdn, vec, part, y, gx)
         dwqkv, dwout, dwup, dwdn, dbqkv, y, gx, g_ln1g, g_ln1b, g_ln2g, g_ln2b, g_bout, g_bdown, g_bup = outs
         dwqkv = jnp.transpose(dwqkv.reshape(nh, 3, head, D), (3, 0, 1, 2))
         dbqkv = jnp.transpose(dbqkv, (1, 0, 2))

time: 67.8 us -> 67 us (0.988)
  Pallas kernels: 66.9 us -> 66.1 us
    pallas_call x1, Pallas kernels: 13.9 us -> 13 us  [local_step(): pl.pallas_call(grad_kernel, name='weight_grads', out_shape=[sds((Q, D), B...]
where the time goes in v6:
time: 67 us; the launch traced here: 66.9 us
  Pallas kernels  66.1 us (99%)
  between operations  0.84 us (1%)
    pallas_call x1, Pallas kernels, local_step(): pl.pallas_call(layer_kernel, name='layer', out_shape=[vm((S // TP, D), BF...  53.1 us
    pallas_call x1, Pallas kernels, local_step(): pl.pallas_call(grad_kernel, name='weight_grads', out_shape=[sds((Q, D), B...  13 us

profile of v6, /device:TPU:0, one launch (start us, length us, event | category | flops | bytes accessed | tf_op | source)
XLA Modules:
  0.0 66.9 jit_solution(3095214081087450479)
XLA Ops:
  0.7 53.1 %layer.1 = (bf16[32,2560]{1,0:T(8,128)(2,1)S(1)}, bf16[32,2560]{1,0:T(8,128)(2,1)S(1)}, f32[7,1,2560]{2,1,0:T(1,128)S(1)}, f32[4,2,2560]{2,1,0:T(2,128)S(1)}, bf...) custom-call(bf16[32,2560]{1,0:T(8,128)(2,1)} %bitcast.13, ...), custom_call_target="tpu_custom_call" | custom-call | tf_op jit(solution)/shard_map/layer/pallas_call | solution.py:554
  53.8 13.0 %weight_grads.1 = (bf16[1920,2560]{1,0:T(8,128)(2,1)}, bf16[640,2560]{1,0:T(8,128)(2,1)}, bf16[2560,2560]{1,0:T(8,128)(2,1)}, bf16[2560,2560]{1,0:T(8,128)(2,1)}...) custom-call(bf16[128,2560]{1,0:T(8,128)(2,1)S(1)} %get-tuple-element, ...), custom_call_target="tpu_custom_call" | custom-call | tf_op jit(solution)/shard_map/weight_grads/pallas_call | solution.py:577

commit v7 on v6

--- a/solution.py
+++ b/solution.py
@@ -58,18 +58,19 @@
     core = lax.rem(t, 2)
     chip = t // 2
     sib = t + 1 - 2 * core
-    cross = lax.rem(t + 2, TP)
-    sibcross = lax.rem(sib + 2, TP)
+    cross = lax.rem(sib + 2, TP)
+    sibcross = lax.rem(t + 2, TP)
+    side = lax.rem(core + chip, 2)
 
     def slot(dev):
-        return lax.rem(dev, 2) * 2 + dev // 2
+        return lax.rem(lax.rem(dev, 2) + dev // 2, 2) * 2 + dev // 2
 
     def rows(dev):
         return pl.ds(pl.multiple_of(slot(dev) * 32, 32), 32)
 
     own = rows(t)
-    half = pl.ds(pl.multiple_of(core * 64, 64), 64)
-    sibhalf = pl.ds(pl.multiple_of((1 - core) * 64, 64), 64)
+    half = pl.ds(pl.multiple_of(side * 64, 64), 64)
+    sibhalf = pl.ds(pl.multiple_of((1 - side) * 64, 64), 64)
     blk_own = pl.ds(pl.multiple_of(chip * 32, 32), 32)
     blk_cross = pl.ds(pl.multiple_of((1 - chip) * 32, 32), 32)
 
@@ -174,7 +175,7 @@
     def position(axis):
         i = lax.broadcasted_iota(jnp.int32, (seq, seq), axis)
         b = i >> 5
-        return ((((b & 1) << 1) | (b >> 1)) << 5) | (i & 31)
+        return ((((b & 1) << 1) | (((b >> 1) ^ b) & 1)) << 5) | (i & 31)
 
     pos_k = position(0)
     causal = pos_k <= position(1)

time: 67 us -> 66.1 us (0.987)
  Pallas kernels: 66.1 us -> 65.2 us
    pallas_call x1, Pallas kernels: 53.1 us -> 52.2 us  [local_step(): pl.pallas_call(layer_kernel, name='layer', out_shape=[vm((S // TP, D), BF...]
where the time goes in v7:
time: 66.1 us; the launch traced here: 66 us
  Pallas kernels  65.2 us (99%)
  between operations  0.84 us (1%)
    pallas_call x1, Pallas kernels, local_step(): pl.pallas_call(layer_kernel, name='layer', out_shape=[vm((S // TP, D), BF...  52.2 us
    pallas_call x1, Pallas kernels, local_step(): pl.pallas_call(grad_kernel, name='weight_grads', out_shape=[sds((Q, D), B...  13 us

profile of v7, /device:TPU:0, one launch (start us, length us, event | category | flops | bytes accessed | tf_op | source)
XLA Modules:
  0.0 66.0 jit_solution(10868267089558392825)
XLA Ops:
  0.7 52.2 %layer.1 = (bf16[32,2560]{1,0:T(8,128)(2,1)S(1)}, bf16[32,2560]{1,0:T(8,128)(2,1)S(1)}, f32[7,1,2560]{2,1,0:T(1,128)S(1)}, f32[4,2,2560]{2,1,0:T(2,128)S(1)}, bf...) custom-call(bf16[32,2560]{1,0:T(8,128)(2,1)} %bitcast.13, ...), custom_call_target="tpu_custom_call" | custom-call | tf_op jit(solution)/shard_map/layer/pallas_call | solution.py:555
  52.9 13.0 %weight_grads.1 = (bf16[1920,2560]{1,0:T(8,128)(2,1)}, bf16[640,2560]{1,0:T(8,128)(2,1)}, bf16[2560,2560]{1,0:T(8,128)(2,1)}, bf16[2560,2560]{1,0:T(8,128)(2,1)}...) custom-call(bf16[128,2560]{1,0:T(8,128)(2,1)S(1)} %get-tuple-element, ...), custom_call_target="tpu_custom_call" | custom-call | tf_op jit(solution)/shard_map/weight_grads/pallas_call | solution.py:578

commit v8 on v7

--- a/solution.py
+++ b/solution.py
@@ -229,9 +229,9 @@
         def step_cross(self, j):
             self.pair(j)
             c = self.ch(j)
-            self.b[j] = remote(self.s.at[:, c], self.rs.at[:, c], cross)
             if j == self.last:
                 self.c[j] = (remote(self.s.at[:, c], self.e.at[:, :], sibcross), remote(self.s.at[:, c], self.q.at[:, :], sib))
+            self.b[j] = remote(self.s.at[:, c], self.rs.at[:, c], cross)
 
         def step_back(self, j):
             self.b[j].wait_recv()
@@ -280,15 +280,29 @@
     lwdn.wait()
     lwup.wait()
     fw = wdn_h.shape[0] // N_BLK
-    acc = jnp.zeros((seq, LANES), F32)
-
-    def x1_chunk(j, acc):
+    shift = None
+    acc1 = jnp.zeros((seq, LANES), F32)
+    acc2 = jnp.zeros((seq, LANES), F32)
+
+    def x1_chunk(j, shift, acc1, acc2):
         sum_a.finish(j)
+        total = jnp.zeros((seq, LANES), F32)
         for c in groups(ALL_CHUNKS, j):
             z = xg[:, lc(c)].astype(F32) + t1[:, lc(c)].astype(F32) + vecs[4, :, lc(c)]
             x1[:, lc(c)] = z
-            acc = acc + z
-        return acc
+            if j == 0:
+                total = total + z
+            else:
+                d = z - shift
+                acc1 = acc1 + d
+                acc2 = acc2 + d * d
+        if j == 0:
+            shift = jnp.sum(total, axis=1, keepdims=True) / (ALL_CHUNKS[0] * LANES)
+            for c in groups(ALL_CHUNKS, j):
+                d = x1[:, lc(c)] - shift
+                acc1 = acc1 + d
+                acc2 = acc2 + d * d
+        return shift, acc1, acc2
 
     gyv = gyg[...]
     for j in range(n_all):
@@ -297,18 +311,14 @@
             gact[:, ff] = dot_t(gyv, wdn[ff, :]).astype(BF)
         sum_a.step_back(j)
         if j:
-            acc = x1_chunk(j - 1, acc)
-    acc = x1_chunk(n_all - 1, acc)
-
-    mean = jnp.sum(acc, axis=1, keepdims=True) / D
+            shift, acc1, acc2 = x1_chunk(j - 1, shift, acc1, acc2)
+    shift, acc1, acc2 = x1_chunk(n_all - 1, shift, acc1, acc2)
+
+    off = jnp.sum(acc1, axis=1, keepdims=True) / D
+    mean = shift + off
+    rstd = lax.rsqrt(jnp.sum(acc2, axis=1, keepdims=True) / D - off * off + EPS)
     halves = (slice(0, seq // 2), slice(seq // 2, seq))
-    rstd2 = []
-    for n, hh in enumerate(halves):
-        acc = jnp.zeros((seq // 2, LANES), F32)
-        for c in range(nlc):
-            z = x1[hh, lc(c)] - mean[hh]
-            acc = acc + z * z
-        rstd2.append(lax.rsqrt(jnp.sum(acc, axis=1, keepdims=True) / D + EPS))
+    rstd2 = [rstd[hh] for hh in halves]
     for n, hh in enumerate(halves):
         for c in range(nlc):
             z = (x1[hh, lc(c)] - mean[hh]) * rstd2[n]
@@ -452,7 +462,7 @@
             acc2 = acc2 + dhz * gain
         if j >= n_scat - 2:
             c = slice(0, sum_h.ch(j).stop) if j == n_scat - 2 else sum_h.ch(j)
-            parts += [remote(part_o.at[me, :, c], part_o.at[me, :, c], dev) for dev in (cross, sibcross, sib)]
+            parts += [remote(part_o.at[me, :, c], part_o.at[me, :, c], dev) for dev in (sibcross, cross, sib)]
     mean1 = jnp.sum(acc1, axis=1, keepdims=True) / D
     mean2 = jnp.sum(acc2, axis=1, keepdims=True) / D
     for c in range(nlc):

time: 66.1 us -> 66.2 us (level)
  no operation moved by 1% of the time
where the time goes in v8:
time: 66.2 us; the launch traced here: 66.1 us
  Pallas kernels  65.2 us (98%)
  between operations  0.84 us (1%)
    pallas_call x1, Pallas kernels, local_step(): pl.pallas_call(layer_kernel, name='layer', out_shape=[vm((S // TP, D), BF...  52.2 us
    pallas_call x1, Pallas kernels, local_step(): pl.pallas_call(grad_kernel, name='weight_grads', out_shape=[sds((Q, D), B...  13 us

profile of v8, /device:TPU:0, one launch (start us, length us, event | category | flops | bytes accessed | tf_op | source)
XLA Modules:
  0.0 66.1 jit_solution(8142674432877849187)
XLA Ops:
  0.7 52.2 %layer.1 = (bf16[32,2560]{1,0:T(8,128)(2,1)S(1)}, bf16[32,2560]{1,0:T(8,128)(2,1)S(1)}, f32[7,1,2560]{2,1,0:T(1,128)S(1)}, f32[4,2,2560]{2,1,0:T(2,128)S(1)}, bf...) custom-call(bf16[32,2560]{1,0:T(8,128)(2,1)} %bitcast.13, ...), custom_call_target="tpu_custom_call" | custom-call | tf_op jit(solution)/shard_map/layer/pallas_call | solution.py:565
  52.9 13.0 %weight_grads.1 = (bf16[1920,2560]{1,0:T(8,128)(2,1)}, bf16[640,2560]{1,0:T(8,128)(2,1)}, bf16[2560,2560]{1,0:T(8,128)(2,1)}, bf16[2560,2560]{1,0:T(8,128)(2,1)}...) custom-call(bf16[128,2560]{1,0:T(8,128)(2,1)S(1)} %get-tuple-element, ...), custom_call_target="tpu_custom_call" | custom-call | tf_op jit(solution)/shard_map/weight_grads/pallas_call | solution.py:588

commit v9 on v8

--- a/solution.py
+++ b/solution.py
@@ -229,9 +229,9 @@
         def step_cross(self, j):
             self.pair(j)
             c = self.ch(j)
+            self.b[j] = remote(self.s.at[:, c], self.rs.at[:, c], cross)
             if j == self.last:
                 self.c[j] = (remote(self.s.at[:, c], self.e.at[:, :], sibcross), remote(self.s.at[:, c], self.q.at[:, :], sib))
-            self.b[j] = remote(self.s.at[:, c], self.rs.at[:, c], cross)
 
         def step_back(self, j):
             self.b[j].wait_recv()
@@ -462,7 +462,7 @@
             acc2 = acc2 + dhz * gain
         if j >= n_scat - 2:
             c = slice(0, sum_h.ch(j).stop) if j == n_scat - 2 else sum_h.ch(j)
-            parts += [remote(part_o.at[me, :, c], part_o.at[me, :, c], dev) for dev in (sibcross, cross, sib)]
+            parts += [remote(part_o.at[me, :, c], part_o.at[me, :, c], dev) for dev in (cross, sibcross, sib)]
     mean1 = jnp.sum(acc1, axis=1, keepdims=True) / D
     mean2 = jnp.sum(acc2, axis=1, keepdims=True) / D
     for c in range(nlc):

time: 66.2 us -> 65.9 us (level)
  no operation moved by 1% of the time
where the time goes in v9:
time: 65.9 us; the launch traced here: 65.8 us
  Pallas kernels  65 us (99%)
  between operations  0.84 us (1%)
    pallas_call x1, Pallas kernels, local_step(): pl.pallas_call(layer_kernel, name='layer', out_shape=[vm((S // TP, D), BF...  52 us
    pallas_call x1, Pallas kernels, local_step(): pl.pallas_call(grad_kernel, name='weight_grads', out_shape=[sds((Q, D), B...  13 us

profile of v9, /device:TPU:0, one launch (start us, length us, event | category | flops | bytes accessed | tf_op | source)
XLA Modules:
  0.0 65.8 jit_solution(18398043696097060369)
XLA Ops:
  0.7 52.0 %layer.1 = (bf16[32,2560]{1,0:T(8,128)(2,1)S(1)}, bf16[32,2560]{1,0:T(8,128)(2,1)S(1)}, f32[7,1,2560]{2,1,0:T(1,128)S(1)}, f32[4,2,2560]{2,1,0:T(2,128)S(1)}, bf...) custom-call(bf16[32,2560]{1,0:T(8,128)(2,1)} %bitcast.13, ...), custom_call_target="tpu_custom_call" | custom-call | tf_op jit(solution)/shard_map/layer/pallas_call | solution.py:565
  52.6 13.0 %weight_grads.1 = (bf16[1920,2560]{1,0:T(8,128)(2,1)}, bf16[640,2560]{1,0:T(8,128)(2,1)}, bf16[2560,2560]{1,0:T(8,128)(2,1)}, bf16[2560,2560]{1,0:T(8,128)(2,1)}...) custom-call(bf16[128,2560]{1,0:T(8,128)(2,1)S(1)} %get-tuple-element, ...), custom_call_target="tpu_custom_call" | custom-call | tf_op jit(solution)/shard_map/weight_grads/pallas_call | solution.py:588

commit v10 on v9

--- a/solution.py
+++ b/solution.py
@@ -24,6 +24,7 @@
 LAYER_VMEM = 47 * 1024 * 1024
 GRAD_VMEM = 24 * 1024 * 1024
 N_REMOTE = 62
+N_SEND = 42
 
 
 def alibi_slopes(n_heads):
@@ -84,15 +85,23 @@
         return copy
 
     sent = []
+    free = list(range(N_SEND))
 
     def remote(src, dst, dev):
         k = counter[1]
         counter[1] += 1
-        copy = pltpu.make_async_remote_copy(src_ref=src, dst_ref=dst, send_sem=ssem.at[k], recv_sem=rsem.at[k],
+        at = free.pop(0)
+        copy = pltpu.make_async_remote_copy(src_ref=src, dst_ref=dst, send_sem=ssem.at[at], recv_sem=rsem.at[k],
                                             device_id={'tp': dev}, device_id_type=MESH)
         copy.start()
-        sent.append(copy)
+        sent.append((copy, at))
         return copy
+
+    def sends_done(n):
+        for copy, at in sent[:n]:
+            copy.wait_send()
+            free.append(at)
+        del sent[:n]
 
     def lc(c):
         return slice(c * LANES, (c + 1) * LANES)
@@ -339,6 +348,7 @@
         dpre[:, ff] = gp.astype(BF)
 
     dv = dpre[...]
+    n_before = len(sent)
     sum_g = AllSum(p2, rd2, s2, rs2, t2, q2, e2)
     for j in range(n_all):
         for c in [lc(c) for c in groups(ALL_CHUNKS, j)] if j == 0 else [sum_g.ch(j)]:
@@ -348,6 +358,7 @@
             sum_g.step_cross(j - 1)
     sum_g.step_cross(n_all - 1)
 
+    sends_done(n_before)
     acc1 = jnp.zeros((seq, LANES), F32)
     acc2 = jnp.zeros((seq, LANES), F32)
 
@@ -425,6 +436,7 @@
         dqkv[part_of(hd, 0), :] = (dot(qkv[part_of(hd, 1), :], dsb[hd]) * score_scale).astype(BF)
         dqkv[part_of(hd, 1), :] = (dot_t(qkv[part_of(hd, 0), :], dsb[hd]) * score_scale).astype(BF)
 
+    n_before = len(sent)
     sum_h = ScatterSum(ph, rdh, sh, rsh, None, None, None)
     n_scat = len(SCATTER_CHUNKS)
     dq = dqkv[...].T
@@ -449,6 +461,7 @@
     parts = []
     for step, m in work[WORK_CUTS[-1]:]:
         step(m)
+    sends_done(n_before)
     for j in range(n_scat):
         sum_h.b[j].wait_recv()
         for c in groups(SCATTER_CHUNKS, j):
@@ -468,8 +481,7 @@
     for c in range(nlc):
         dz = sum_h.result(lc(c)) * vecs[0, :, lc(c)]
         gxbuf[:, lc(c)] = (gmid[own, lc(c)] + rstd1 * (dz - mean1 - xh1[:, lc(c)] * mean2)).astype(BF)
-    for copy in sent:
-        copy.wait_send()
+    sends_done(len(sent))
     for copy in parts:
         copy.wait_recv()
 
@@ -578,7 +590,7 @@
                 vm((nh, S, head), BF), vm((nh, S, S), BF), vm((nh, S, S), BF),
                 *red, *red, *scat, *scat,
                 pltpu.SemaphoreType.DMA((n_loads,)),
-                pltpu.SemaphoreType.DMA((N_REMOTE,)), pltpu.SemaphoreType.DMA((N_REMOTE,)),
+                pltpu.SemaphoreType.DMA((N_SEND,)), pltpu.SemaphoreType.DMA((N_REMOTE,)),
             ],
             compiler_params=pltpu.CompilerParams(collective_id=0, has_side_effects=True, vmem_limit_bytes=LAYER_VMEM),
         )(x.reshape(x.shape[1], D), grad_y.reshape(x.shape[1], D), wqkv_t, bq, w_out, w_up, w_down, row(ln1_gamma), row(ln1_beta),

time: 65.9 us -> 65.8 us (level)
  no operation moved by 1% of the time
where the time goes in v10:
time: 65.8 us; the launch traced here: 65.7 us
  Pallas kernels  64.8 us (98%)
  between operations  0.84 us (1%)
    pallas_call x1, Pallas kernels, local_step(): pl.pallas_call(layer_kernel, name='layer', out_shape=[vm((S // TP, D), BF...  51.8 us
    pallas_call x1, Pallas kernels, local_step(): pl.pallas_call(grad_kernel, name='weight_grads', out_shape=[sds((Q, D), B...  13 us

profile of v10, /device:TPU:0, one launch (start us, length us, event | category | flops | bytes accessed | tf_op | source)
XLA Modules:
  0.0 65.7 jit_solution(13112528210500510745)
XLA Ops:
  0.7 51.8 %layer.1 = (bf16[32,2560]{1,0:T(8,128)(2,1)S(1)}, bf16[32,2560]{1,0:T(8,128)(2,1)S(1)}, f32[7,1,2560]{2,1,0:T(1,128)S(1)}, f32[4,2,2560]{2,1,0:T(2,128)S(1)}, bf...) custom-call(bf16[32,2560]{1,0:T(8,128)(2,1)} %bitcast.13, ...), custom_call_target="tpu_custom_call" | custom-call | tf_op jit(solution)/shard_map/layer/pallas_call | solution.py:577
  52.5 13.0 %weight_grads.1 = (bf16[1920,2560]{1,0:T(8,128)(2,1)}, bf16[640,2560]{1,0:T(8,128)(2,1)}, bf16[2560,2560]{1,0:T(8,128)(2,1)}, bf16[2560,2560]{1,0:T(8,128)(2,1)}...) custom-call(bf16[128,2560]{1,0:T(8,128)(2,1)S(1)} %get-tuple-element, ...), custom_call_target="tpu_custom_call" | custom-call | tf_op jit(solution)/shard_map/weight_grads/pallas_call | solution.py:600

commit v11 on v10

--- a/solution.py
+++ b/solution.py
@@ -17,7 +17,7 @@
 TP = 4
 LANES = 128
 ALL_CHUNKS = (2, 4, 4, 5, 4, 1)
-SCATTER_CHUNKS = (2, 6, 8, 4)
+SCATTER_CHUNKS = (2, 8, 8, 2)
 N_BLK = 5
 GRAD_ROWS = 640
 WORK_CUTS = (0, 3, 5, 6, 7, 7, 7)

time: 65.8 us -> 65.9 us (level)
  no operation moved by 1% of the time
where the time goes in v11:
time: 65.9 us; the launch traced here: 65.8 us
  Pallas kernels  65 us (99%)
  between operations  0.84 us (1%)
    pallas_call x1, Pallas kernels, local_step(): pl.pallas_call(layer_kernel, name='layer', out_shape=[vm((S // TP, D), BF...  52 us
    pallas_call x1, Pallas kernels, local_step(): pl.pallas_call(grad_kernel, name='weight_grads', out_shape=[sds((Q, D), B...  13 us

profile of v11, /device:TPU:0, one launch (start us, length us, event | category | flops | bytes accessed | tf_op | source)
XLA Modules:
  0.0 65.8 jit_solution(613745751145655531)
XLA Ops:
  0.7 52.0 %layer.1 = (bf16[32,2560]{1,0:T(8,128)(2,1)S(1)}, bf16[32,2560]{1,0:T(8,128)(2,1)S(1)}, f32[7,1,2560]{2,1,0:T(1,128)S(1)}, f32[4,2,2560]{2,1,0:T(2,128)S(1)}, bf...) custom-call(bf16[32,2560]{1,0:T(8,128)(2,1)} %bitcast.13, ...), custom_call_target="tpu_custom_call" | custom-call | tf_op jit(solution)/shard_map/layer/pallas_call | solution.py:577
  52.7 13.0 %weight_grads.1 = (bf16[1920,2560]{1,0:T(8,128)(2,1)}, bf16[640,2560]{1,0:T(8,128)(2,1)}, bf16[2560,2560]{1,0:T(8,128)(2,1)}, bf16[2560,2560]{1,0:T(8,128)(2,1)}...) custom-call(bf16[128,2560]{1,0:T(8,128)(2,1)S(1)} %get-tuple-element, ...), custom_call_target="tpu_custom_call" | custom-call | tf_op jit(solution)/shard_map/weight_grads/pallas_call | solution.py:600
